TPU v7x, 32 devices: a whole 2x2x4 slice. The times are simulated.
32 devices in a mesh: gx: 4 (over z), gy: 8 (over y, x, core).
Axes of the slice: x: 2, y: 2, z: 4, core: 2. Of those that a mesh axis runs over, the one named last changes fastest.
Arguments:
- item_table: bfloat16 [262144, 256], P(('gx', 'gy')), may hold values from -0.625 to 0.625
- bilinear: bfloat16 [256, 1024], replicated, may hold values from -0.375 to 0.375
- requests: int32 [32, 32, 64], P(('gx', 'gy')), may hold values from -1 to 8191, as said below
- history: int32 [8192, 50], P(('gx', 'gy')), may hold values from 0 to 2047, as said below
- lengths: int32 [8192], P(('gx', 'gy')), may hold values from 10 to 50
- init_logits: float32 [8192, 50, 4], P(('gx', 'gy')), may hold values from -6 to 6
- interest_grad: float32 [8192, 4, 256], P(('gx', 'gy')), may hold values from -6 to 6
Outputs:
- interests: bfloat16 [8192, 4, 256], P(('gx', 'gy'))
- table_grad: float32 [262144, 256], P(('gx', 'gy'))
Inputs may be any that keep to these rules, and one draw needn't show every extreme that they name: requests[r, o, c] is a row of table shard o asked by device r in slot c, or -1 for an unused slot; the used slots of a list come first, hold distinct rows, and number at least one; a few shards have full lists (64 used slots) from every device. history[u, l] = o * 64 + c names a used slot c of list o of the device holding user u (users are laid out 256 a device).
All inputs are finite; a program needn't handle non-finite values.
Results may differ from a plain program's by a relative error of at most 0.015.
Values may be sent and summed in bfloat16 or wider, within the bound.
No kernel may reach another device: no remote copies, remote signals or barrier semaphores. Data moves between devices by JAX's collectives and lax.ppermute only.
A program may use at most 192 MiB of HBM per device.

v0:
```python
import jax
import jax.numpy as jnp
from jax import lax
from jax.sharding import PartitionSpec as P

ITERS = 3


squash_eps = 1e-06


def route_interests(behavior_rows, bilinear, lengths, init_logits):
    users_here, hist_count, feature_width = behavior_rows.shape
    interest_count = init_logits.shape[2]
    remapped_values = jnp.dot(
        behavior_rows.reshape(users_here * hist_count, feature_width),
        bilinear,
        preferred_element_type=jnp.float32,
    )
    remapped_values = remapped_values.astype(jnp.bfloat16).reshape(
        users_here, hist_count, interest_count, feature_width
    )
    positions = lax.broadcasted_iota(jnp.int32, (users_here, hist_count), 1)
    live_mask = (positions < lengths[:, None]).astype(jnp.float32)
    logits = init_logits
    interest_capsule = None
    for turn_no in range(ITERS):
        exponent = jnp.exp(logits)
        coupling_weight = (
            exponent / jnp.sum(exponent, axis=2, keepdims=True) * live_mask[:, :, None]
        )
        weighted_total = jnp.einsum(
            "rmq,rmqs->rqs",
            coupling_weight.astype(jnp.bfloat16),
            remapped_values,
            preferred_element_type=jnp.float32,
        )
        norm_sq = jnp.sum(weighted_total * weighted_total, axis=2, keepdims=True)
        interest_capsule = weighted_total * jnp.sqrt(norm_sq + squash_eps) / (1.0 + norm_sq)
        if turn_no + 1 < ITERS:
            routing_agreement_score = jnp.einsum(
                "mazc,mzc->maz",
                remapped_values,
                interest_capsule.astype(jnp.bfloat16),
                preferred_element_type=jnp.float32,
            )
            logits = logits + routing_agreement_score
    return interest_capsule


def local(item_table, bilinear, requests, history, lengths, init_logits, interest_grad):
    asked_ids = requests[0]
    owner_count, slot_count = asked_ids.shape
    local_table_rows, feature_width = item_table.shape
    wanted = lax.all_to_all(asked_ids, ("gx", "gy"), split_axis=0, concat_axis=0, tiled=True)
    found = jnp.take(item_table, jnp.maximum(wanted, 0).reshape(-1), axis=0).reshape(
        owner_count, slot_count, feature_width
    )
    fetched = lax.all_to_all(found, ("gx", "gy"), split_axis=0, concat_axis=0, tiled=True)
    fetched = fetched.reshape(owner_count * slot_count, feature_width)
    slot_flat = history.reshape(-1)
    behavior_rows = jnp.take(fetched, slot_flat, axis=0).reshape(
        history.shape[0], history.shape[1], feature_width
    )
    interest_capsule, pullback = jax.vjp(
        lambda given: route_interests(given, bilinear, lengths, init_logits), behavior_rows
    )
    (row_grad,) = pullback(interest_grad)
    slot_grads = jax.ops.segment_sum(
        row_grad.reshape(-1, feature_width).astype(jnp.float32),
        slot_flat,
        num_segments=owner_count * slot_count,
    )
    returned = lax.all_to_all(
        slot_grads.reshape(owner_count, slot_count, feature_width).astype(jnp.bfloat16),
        ("gx", "gy"),
        split_axis=0,
        concat_axis=0,
        tiled=True,
    ).astype(jnp.float32)
    returned = returned.reshape(owner_count * slot_count, feature_width)
    targets = jnp.where(wanted >= 0, wanted, local_table_rows).reshape(-1)
    table_grad = jax.ops.segment_sum(returned, targets, num_segments=local_table_rows + 1)[
        :local_table_rows
    ]
    return (interest_capsule.astype(jnp.bfloat16), table_grad)


def solution(mesh):
    placed = (
        P(("gx", "gy"), None),
        P(),
        P(("gx", "gy"), None, None),
        P(("gx", "gy"), None),
        P(("gx", "gy")),
        P(("gx", "gy"), None, None),
        P(("gx", "gy"), None, None),
    )
    return jax.shard_map(
        local,
        mesh=mesh,
        in_specs=placed,
        out_specs=(P(("gx", "gy"), None, None), P(("gx", "gy"), None)),
        check_vma=False,
    )
```

profile of v0, /device:TPU:0, one launch (start us, length us, event | category | flops | bytes accessed | tf_op | source)
XLA Modules:
  0.0 600.2 jit_solution(7761657087312523334)
XLA Ops:
  0.6 14.4 %all_to_all.22 = s32[32,1,64]{2,1,0:T(1,128)S(1)} all-to-all(s32[32,1,64]{2,1,0:T(1,128)} %bitcast.191), channel_id=1, replica_groups=mesh['gx'=4,'gy'=8] {'gx','gy'}, dimensions={0} | all-to-all | bytes 16384 | tf_op jit(solution)/shard_map/all_to_all | solution.py:55
  17.0 9.4 %gather_fusion = bf16[2048,256]{1,0:T(8,128)(2,1)S(1)} fusion(bf16[8192,256]{1,0:T(8,128)(2,1)} %param.7, s32[2048]{0:T(1024)S(1)} %broadcast_clamp_fusion), kind=kCustom, calls=%fused_computation | custom fusion | bytes 2105344 | tf_op jit(solution)/shard_map/jit(_take)/gather | solution.py:56
  41.6 14.8 %all-to-all-done.1 = bf16[32,64,256]{2,1,0:T(8,128)(2,1)S(1)} async-done(((bf16[32,64,256]{2,1,0:T(8,128)(2,1)}), bf16[32,64,256]{2,1,0:T(8,128)(2,1)S(1)}, u32[]{:S(2)}, u32[]{:S(2)}) %all-to-all-start.1) | async-done | bytes 1048608 | tf_op jit(solution)/shard_map/all_to_all | solution.py:59
  56.5 36.0 %gather_fusion.1 = bf16[12800,256]{1,0:T(8,128)(2,1)} fusion(bf16[2048,256]{1,0:T(8,128)(2,1)S(1)} %bitcast.172, s32[13312]{0:T(1024)S(1)} %pad_clamp_fusion), kind=kCustom, calls=%fused_computation.1 | custom fusion | bytes 13158400 | tf_op jit(solution)/shard_map/jit(_take)/gather | solution.py:62
  92.4 15.6 %convolution_convert_fusion = bf16[12800,1024]{1,0:T(8,128)(2,1)} fusion(bf16[256,1024]{1,0:T(8,128)(2,1)S(1)} %copy-done, bf16[12800,256]{1,0:T(8,128)(2,1)} %gather_fusion.1, pred[12800]{0:T(1024)(128)(4,1)S(1)} %compare_and_fusion), kind=kOutput, calls=%fused_computation.19 | convolution fusion | flops 6727270400 | bytes 33305088 | tf_op jit(solution)/shard_map/jvp()/dot_general | solution.py:15
  108.0 43.0 %reshape.235 = bf16[256,50,4,256]{3,2,1,0:T(4,128)(2,1)} reshape(bf16[12800,1024]{1,0:T(8,128)(2,1)} %convolution_convert_fusion) | data formatting | bytes 52428800 | tf_op jit(solution)/shard_map/jvp()/reshape | solution.py:20
  151.0 13.6 %fusion.27 = f32[256,4,1,256]{3,2,1,0:T(1,128)S(1)} fusion(bf16[256,50,4,1]{1,3,2,0:T(2,128)(2,1)S(1)} %copy.79, bf16[256,50,4,256]{3,2,1,0:T(4,128)(2,1)} %reshape.235), kind=kOutput, calls=%fused_computation.38 | convolution fusion | flops 26214400 | bytes 27365376 | tf_op jit(solution)/shard_map/jvp(rmq,rmqs->rqs)/dot_general | solution.py:32
  167.4 13.0 %fusion.25 = f32[256,4,1,50]{3,2,1,0:T(1,128)S(1)} fusion(bf16[256,50,4,256]{3,2,1,0:T(4,128)(2,1)} %reshape.235, bf16[256,4,256,1]{2,1,0,3:T(4,128)(2,1)S(1)} %bitcast.184), kind=kOutput, calls=%fused_computation.36 | convolution fusion | flops 26214400 | bytes 26943488 | tf_op jit(solution)/shard_map/jvp(mazc,mzc->maz)/dot_general | solution.py:41
  183.6 13.7 %fusion.23 = f32[256,4,1,256]{3,2,1,0:T(1,128)S(1)} fusion(bf16[256,50,4,1]{1,3,2,0:T(2,128)(2,1)} %copy.84, bf16[256,50,4,256]{3,2,1,0:T(4,128)(2,1)} %reshape.235), kind=kOutput, calls=%fused_computation.34 | convolution fusion | flops 26214400 | bytes 27365376 | tf_op jit(solution)/shard_map/jvp(rmq,rmqs->rqs)/dot_general | solution.py:32
  200.1 13.6 %fusion.21 = f32[256,4,1,50]{3,2,1,0:T(1,128)} fusion(bf16[256,50,4,256]{3,2,1,0:T(4,128)(2,1)} %reshape.235, bf16[256,4,256,1]{2,1,0,3:T(4,128)(2,1)S(1)} %bitcast.185), kind=kOutput, calls=%fused_computation.32 | convolution fusion | flops 26214400 | bytes 26943488 | tf_op jit(solution)/shard_map/jvp(mazc,mzc->maz)/dot_general | solution.py:41
  219.6 13.7 %fusion.19 = f32[256,4,1,256]{3,2,1,0:T(1,128)S(1)} fusion(bf16[256,50,4,1]{1,3,2,0:T(2,128)(2,1)} %copy.88, bf16[256,50,4,256]{3,2,1,0:T(4,128)(2,1)} %reshape.235), kind=kOutput, calls=%fused_computation.30 | convolution fusion | flops 26214400 | bytes 27365376 | tf_op jit(solution)/shard_map/jvp(rmq,rmqs->rqs)/dot_general | solution.py:32
  246.1 13.5 %fusion.17 = bf16[256,4,1,50]{3,2,1,0:T(2,128)(2,1)} fusion(bf16[256,50,4,256]{3,2,1,0:T(4,128)(2,1)} %reshape.235, f32[256,4,256,1]{2,1,0,3:T(4,128)S(1)} %bitcast.176), kind=kOutput, calls=%fused_computation.28 | convolution fusion | flops 26214400 | bytes 27365376 | tf_op jit(solution)/shard_map/transpose(jvp(rmq,rmqs->rqs))/dot_general | solution.py:32
  263.9 13.9 %fusion.15 = bf16[256,4,1,256]{3,2,1,0:T(2,128)(2,1)S(1)} fusion(bf16[256,4,50,1]{2,3,1,0:T(2,128)(2,1)} %copy.92, bf16[256,50,4,256]{3,2,1,0:T(4,128)(2,1)} %reshape.235), kind=kOutput, calls=%fused_computation.26 | convolution fusion | flops 26214400 | bytes 26841088 | tf_op jit(solution)/shard_map/transpose(jvp(mazc,mzc->maz))/dot_general | solution.py:41
  293.6 12.8 %fusion.13 = bf16[256,4,1,50]{3,2,1,0:T(2,128)(2,1)S(1)} fusion(bf16[256,50,4,256]{3,2,1,0:T(4,128)(2,1)} %reshape.235, f32[256,4,256,1]{2,1,0,3:T(4,128)S(1)} %bitcast.175), kind=kOutput, calls=%fused_computation.24 | convolution fusion | flops 26214400 | bytes 27365376 | tf_op jit(solution)/shard_map/transpose(jvp(rmq,rmqs->rqs))/dot_general | solution.py:32
  309.3 13.8 %fusion.11 = bf16[256,4,1,256]{3,2,1,0:T(2,128)(2,1)S(1)} fusion(bf16[256,4,50,1]{2,3,1,0:T(2,128)(2,1)S(1)} %copy.96, bf16[256,50,4,256]{3,2,1,0:T(4,128)(2,1)} %reshape.235), kind=kOutput, calls=%fused_computation.22 | convolution fusion | flops 26214400 | bytes 26841088 | tf_op jit(solution)/shard_map/transpose(jvp(mazc,mzc->maz))/dot_general | solution.py:41
  323.1 8.2 %fusion.41 = (f32[256,4]{1,0:T(8,128)S(1)}, f32[256,4]{1,0:T(8,128)S(1)}) fusion(f32[256,4,1,256]{3,2,1,0:T(1,128)S(1)} %fusion.27, f32[256,4]{1,0:T(8,128)} %get-tuple-element.26, f32[256,4]{1,0:T(8,128)} %copy-done.8, bf16[256,4,1,256]{3,2,1,0:T(2,128)(2,1)S(1)} %fusion.11, f32[256,4]{1,0:T(8,128)} %copy-done.7), kind=kLoop, calls=%fused_computation.59 | loop fusion | flops 2095104 | bytes 1593344 | tf_op jit(solution)/shard_map/transpose(jvp())/reduce_sum | solution.py:39
  335.0 8.4 %copy.68 = f32[256,4,50]{1,2,0:T(8,128)} copy(f32[256,4,50]{0,1,2:T(4,128)} %get-tuple-element.8) | data formatting | bytes 409600 | tf_op jit(solution)/shard_map/convert.8
  343.4 8.2 %copy.73 = f32[256,4,50]{1,2,0:T(8,128)} copy(f32[256,4,50]{0,1,2:T(4,128)} %get-tuple-element.12) | data formatting | bytes 409600 | tf_op jit(solution)/shard_map/convert.9
  366.9 77.3 %fusion.5 = bf16[256,50,4,256]{3,2,1,0:T(4,128)(2,1)} fusion(f32[256,4,50]{1,2,0:T(8,128)} %copy.78, f32[256,4,256]{2,1,0:T(4,128)S(1)} %copy-done.5, f32[256,4,256]{2,1,0:T(4,128)} %get-tuple-element.14, f32[256,4,50]{1,2,0:T(8,128)} %copy.74, f32[256,4,50]{1,2,0:T(8,128)} %copy.73, f32[256,4,256]{2,1,0:T(4,128)S(1)} %copy-done.4, ...), kind=kLoop, calls=%fused_computation.14 | loop fusion | flops 183500800 | bytes 32481280 | tf_op jit(solution)/shard_map/transpose(jvp(rmq,rmqs->rqs))/add_any | solution.py:32
  444.3 18.4 %copy.98 = bf16[1600,8,4,256]{3,1,2,0:T(8,128)(2,1)} copy(bf16[1600,8,4,256]{3,2,1,0:T(4,128)(2,1)} %bitcast.173) | data formatting | bytes 52428800
  462.7 14.8 %fusion.10 = f32[12800,256]{1,0:T(8,128)} fusion(bf16[12800,1024]{1,0:T(8,128)(2,1)} %bitcast.174, bf16[256,1024]{1,0:T(8,128)(2,1)S(1)} %copy-done), kind=kOutput, calls=%fused_computation.21 | convolution fusion | flops 6717440000 | bytes 39845888 | tf_op jit(solution)/shard_map/transpose(jvp())/dot_general | solution.py:15
  477.4 69.6 %scatter_custom_fusion = f32[2048,256]{1,0:T(8,128)S(1)} fusion(s32[12800]{0:T(1024)} %copy-done.17, f32[12800,256]{1,0:T(8,128)} %fusion.10, f32[]{:T(128)} %constant.21.clone.1), kind=kCustom, calls=%fused_computation.85 | custom fusion | flops 3276800 | bytes 2097664 | tf_op jit(solution)/shard_map/scatter-add | solution.py:69
  547.1 29.5 %all_to_all.23 = bf16[32,64,256]{2,1,0:T(8,128)(2,1)S(1)} all-to-all(bf16[32,64,256]{2,1,0:T(8,128)(2,1)S(1)} %bitcast.177), channel_id=1, replica_groups=mesh['gx'=4,'gy'=8] {'gx','gy'}, dimensions={0} | all-to-all | bytes 2097152 | tf_op jit(solution)/shard_map/all_to_all | solution.py:74
  576.7 15.8 %scatter_custom_fusion.1 = f32[8193,256]{1,0:T(8,128)} fusion(s32[2048]{0:T(1024)} %bitcast.192, f32[]{:T(128)} %constant.21.clone.1, bf16[2048,256]{1,0:T(8,128)(2,1)S(1)} %bitcast.178), kind=kCustom, calls=%fused_computation.42 | custom fusion | flops 1048576 | bytes 9438720 | tf_op jit(solution)/shard_map/scatter-add | solution.py:83
  (119 shorter events, 93.8 us)
Async XLA Ops:
  0.6 91.8 %copy-start = (bf16[256,1024]{1,0:T(8,128)(2,1)S(1)}, bf16[256,1024]{1,0:T(8,128)(2,1)}, u32[]{:S(2)}) copy-start(bf16[256,1024]{1,0:T(8,128)(2,1)} %param.8) | copy-start | bytes 1572868
  27.6 28.8 %all-to-all-start.1 = ((bf16[32,64,256]{2,1,0:T(8,128)(2,1)}), bf16[32,64,256]{2,1,0:T(8,128)(2,1)S(1)}, u32[]{:S(2)}, u32[]{:S(2)}) async-start(bf16[32,64,256]{2,1,0:T(8,128)(2,1)} %broadcast_select_fusion), calls=%async_computation.1 | async-start | bytes 2097152 | tf_op jit(solution)/shard_map/all_to_all | solution.py:59
  31.5 60.9 %copy-start.17 = (s32[12800]{0:T(1024)}, s32[12800]{0:T(1024)S(1)}, u32[]{:S(2)}) copy-start(s32[12800]{0:T(1024)S(1)} %reshape.232) | copy-start | bytes 153604
  164.6 16.2 %copy-start.18 = (f32[256,50,4]{0,2,1:T(4,128)S(1)}, f32[256,50,4]{0,2,1:T(4,128)}, u32[]{:S(2)}) copy-start(f32[256,50,4]{0,2,1:T(4,128)} %param.12) | copy-start | bytes 614404
  165.0 2.4 copy-start.19
  165.7 16.7 %copy-start.7 = (f32[256,4]{1,0:T(8,128)}, f32[256,4]{1,0:T(8,128)S(1)}, u32[]{:S(2)}) copy-start(f32[256,4]{1,0:T(8,128)S(1)} %get-tuple-element.27) | copy-start | bytes 12292
  165.9 16.5 %copy-start.8 = (f32[256,4]{1,0:T(8,128)}, f32[256,4]{1,0:T(8,128)S(1)}, u32[]{:S(2)}) copy-start(f32[256,4]{1,0:T(8,128)S(1)} %copy.60) | copy-start | bytes 12292
  181.0 2.6 copy-start.12
  197.7 19.9 %copy-start.20 = (f32[256,4]{0,1:T(4,128)}, f32[256,4]{0,1:T(4,128)S(1)}, u32[]{:S(2)}) copy-start(f32[256,4]{0,1:T(4,128)S(1)} %copy.61) | copy-start | bytes 12292
  217.0 2.6 copy-start.14
  233.3 1.0 copy-start.1
  234.2 26.7 %copy-start.16 = (f32[256,50]{0,1:T(8,128)S(1)}, f32[256,50]{0,1:T(8,128)}, u32[]{:S(2)}) copy-start(f32[256,50]{0,1:T(8,128)} %multiply_divide_fusion.4) | copy-start | bytes 153604
  245.1 1.0 copy-start.6
  260.9 0.6 copy-start.11
  263.9 14.8 %copy-start.15 = (f32[256,4]{1,0:T(8,128)S(1)}, f32[256,4]{1,0:T(8,128)}, u32[]{:S(2)}) copy-start(f32[256,4]{1,0:T(8,128)} %get-tuple-element.22) | copy-start | bytes 12292
  277.8 1.0 copy-start.2
  277.8 30.1 %copy-start.13 = (f32[256,50]{0,1:T(8,128)S(1)}, f32[256,50]{0,1:T(8,128)}, u32[]{:S(2)}) copy-start(f32[256,50]{0,1:T(8,128)} %copy-done.12) | copy-start | bytes 153604
  292.7 1.0 copy-start.3
  308.0 0.7 copy-start.9
  309.3 42.3 %copy-start.10 = (f32[256,50,4]{0,2,1:T(4,128)S(1)}, f32[256,50,4]{0,2,1:T(4,128)}, u32[]{:S(2)}) copy-start(f32[256,50,4]{0,2,1:T(4,128)} %copy-done.9) | copy-start | bytes 614404
  335.0 32.0 %copy-start.4 = (f32[256,4,256]{2,1,0:T(4,128)S(1)}, f32[256,4,256]{2,1,0:T(4,128)}, u32[]{:S(2)}) copy-start(f32[256,4,256]{2,1,0:T(4,128)} %copy-done.3) | copy-start | bytes 3145732
  335.0 32.0 %copy-start.5 = (f32[256,4,256]{2,1,0:T(4,128)S(1)}, f32[256,4,256]{2,1,0:T(4,128)}, u32[]{:S(2)}) copy-start(f32[256,4,256]{2,1,0:T(4,128)} %add_add_fusion) | copy-start | bytes 3145732
where the time goes:
time: 612 us; the launch traced here: 600 us
  other arithmetic  210 us (34%)
  local copies, waits for them, and re-layouts  176 us (29%)
  matrix products  152 us (25%)
  blocking collectives  44 us (7%)
  waiting for transfers between devices  14.8 us (2%)
    add_any x1, other arithmetic, route_interests(): jnp.einsum('rmq,rmqs->rqs', coupling_weight.astype(jnp.bfloat16), remappe...  77.3 us
    scatter-add x1, other arithmetic, local(): jax.ops.segment_sum(row_grad.reshape(-1, feature_width).astype(jnp.float3...  69.6 us
    dot_general x5, matrix products, route_interests(): jnp.einsum('rmq,rmqs->rqs', coupling_weight.astype(jnp.bfloat16), remappe...  67.3 us
    dot_general x4, matrix products, route_interests(): jnp.einsum('mazc,mzc->maz', remapped_values, interest_capsule.astype(jnp....  54.3 us
    reshape x1, local copies, waits for them, and re-layouts, route_interests(): remapped_values.astype(jnp.bfloat16)  43 us
    gather x1, local copies, waits for them, and re-layouts, local(): jnp.take(fetched, slot_flat, axis=0)  36 us
    dot_general x2, matrix products, route_interests(): jnp.dot(behavior_rows.reshape(users_here * hist_count, feature_width), bi...  30.3 us
    all_to_all x1, blocking collectives, local(): lax.all_to_all(slot_grads.reshape(owner_count, slot_count, feature_width)...  29.5 us
  transfers between devices with their start and end apart: 1, of which 1 were waited for; matrix products, arithmetic and copies ran while one was open for 2% of the time, Pallas kernels for 0%

commit v1 on v0

v1 whole, which is shorter than its diff:
```python
import functools

import jax
import jax.numpy as jnp
from jax import lax
from jax.experimental import pallas as pl
from jax.experimental.pallas import tpu as pltpu
from jax.sharding import PartitionSpec as P

ITERS = 3
squash_eps = 1e-06
AXES = ("gx", "gy")
BLOCK_USERS = 64
TILE_POSITIONS = 4
f32 = jnp.float32
bf16 = jnp.bfloat16


def dot(a, b):
    return jnp.dot(a, b, preferred_element_type=f32)


def routing_kernel(
    interest_count, tile_count,
    fetched_ref, bil_ref, bilt_ref, owner_ref, slot_ref, lens_ref, logit_ref, cot_ref,
    interests_ref, slotgrad_ref,
    fetched_t, x_ref, xt_ref, lo_ref, oht_a, oht_b, mcat, vcat, stack, rg_ref, oh_rows, rows_a, slot_acc,
):
    slots, width = fetched_ref.shape
    tiles, lanes = owner_ref.shape
    block_count = tiles // tile_count
    cap = lo_ref.shape[1]
    owners = slots // cap
    users = BLOCK_USERS

    for c in range(0, slots, 256):
        fetched_t[:, c:c + 256] = fetched_ref[c:c + 256, :].T

    slot_iota = lax.broadcasted_iota(jnp.int32, (cap, lanes), 0)

    def indicator(orow16, o):
        return jnp.where(orow16 == o, 1.0, 0.0).astype(bf16)

    def build(tile, buf):
        crow = slot_ref[pl.ds(tile, 1), :]
        orow16 = jnp.broadcast_to(owner_ref[pl.ds(tile, 1), :], (16, lanes))
        lo = jnp.where(slot_iota == crow, 1.0, 0.0).astype(bf16)
        lo_ref[tile] = lo
        lo3 = lo.reshape(cap // 16, 16, lanes)

        for o in range(owners):
            buf[o * cap:(o + 1) * cap, :] = (lo3 * indicator(orow16, o)[None]).reshape(cap, lanes)

    def gather(tile, buf):
        xt = dot(fetched_t[...], buf[...])
        xtb = xt.astype(bf16)
        xt_ref[tile] = xtb
        x_ref[tile] = xtb.T

    build(0, oht_a)

    def gather_pair(i, carry):
        t = 2 * i
        build(t + 1, oht_b)
        gather(t, oht_a)
        build(jnp.minimum(t + 2, tiles - 1), oht_a)
        gather(t + 1, oht_b)
        return carry

    lax.fori_loop(0, tiles // 2, gather_pair, 0)

    row_iota = lax.broadcasted_iota(jnp.int32, (users, lanes), 0)
    lane_iota = lax.broadcasted_iota(jnp.int32, (users, lanes), 1)
    diag = (lane_iota % users) == row_iota
    lane_k = lax.broadcasted_iota(jnp.int32, (width, lanes), 1) // users
    padded = logit_ref.shape[1]
    half = lanes // 2

    def over_interests(v):
        s = v[:, :half] + v[:, half:]
        s = s + pltpu.roll(s, users, 1)
        return jnp.concatenate([s, s], axis=1)

    def spread(coef, j):
        rows_a[...] = coef
        for l in range(tile_count * TILE_POSITIONS):
            row = jnp.broadcast_to(rows_a[l:l + 1, :], (users, lanes))
            mcat[l * users:(l + 1) * users, j * lanes:(j + 1) * lanes] = jnp.where(diag, row, 0.0).astype(bf16)

    def weighted_sum(b, j):
        total = jnp.zeros((width, lanes), f32)
        for t in range(tile_count):
            total = total + dot(
                xt_ref[b * tile_count + t],
                mcat[t * lanes:(t + 1) * lanes, j * lanes:(j + 1) * lanes],
            )
        return total

    def agreement(b, vec):
        for t in range(tile_count):
            prod = dot(x_ref[b * tile_count + t], vec)
            for p in range(TILE_POSITIONS):
                part = jnp.where(diag, prod[p * users:(p + 1) * users, :], 0.0)
                l = t * TILE_POSITIONS + p
                rows_a[l:l + 1, :] = jnp.sum(part, axis=0, keepdims=True)
        return rows_a[...]

    def by_interest(mat_ref, v):
        vb = v.astype(bf16)
        zero = jnp.zeros_like(v)
        for k in range(interest_count):
            stack[k * width:(k + 1) * width, :] = jnp.where(lane_k == k, v, zero).astype(bf16)
        return dot(mat_ref[...], stack[...])

    def squash(s):
        n = jnp.sum(s * s, axis=0, keepdims=True)
        root = jnp.sqrt(n + squash_eps)
        return n, root, root / (1.0 + n)

    def squash_back(s, dc):
        n, root, fac = squash(s)
        slope = (0.5 * (1.0 + n) / root - root) / ((1.0 + n) * (1.0 + n))
        inner = jnp.sum(dc * s, axis=0, keepdims=True)
        return dc * fac + s * (2.0 * slope * inner)

    slot_acc[...] = jnp.zeros_like(slot_acc)
    pos_iota = lax.broadcasted_iota(jnp.int32, (padded, lanes), 0)

    def per_block(b, carry):
        live = pos_iota < lens_ref[pl.ds(b, 1), :]

        def softmax(v):
            e = jnp.exp(v)
            return e / over_interests(e)

        def keep_vec(vec_t, j):
            vb = vec_t.astype(bf16)
            vcat[j * lanes:(j + 1) * lanes, :] = vb.T
            return vb

        logit1 = logit_ref[b]
        p1 = softmax(logit1)
        spread(jnp.where(live, p1, 0.0), 0)
        s1 = by_interest(bilt_ref, weighted_sum(b, 0))
        c1 = s1 * squash(s1)[2]
        u1 = keep_vec(by_interest(bil_ref, c1), 3)
        logit2 = logit1 + agreement(b, u1)
        p2 = softmax(logit2)
        spread(jnp.where(live, p2, 0.0), 1)
        s2 = by_interest(bilt_ref, weighted_sum(b, 1))
        c2 = s2 * squash(s2)[2]
        u2 = keep_vec(by_interest(bil_ref, c2), 4)
        logit3 = logit2 + agreement(b, u2)
        p3 = softmax(logit3)
        spread(jnp.where(live, p3, 0.0), 2)
        s3 = by_interest(bilt_ref, weighted_sum(b, 2))
        c3 = s3 * squash(s3)[2]
        interests_ref[b] = c3.astype(bf16).T
        ds3 = squash_back(s3, cot_ref[b])
        v3 = keep_vec(by_interest(bil_ref, ds3), 2)
        dp3 = jnp.where(live, agreement(b, v3), 0.0)
        dl3 = p3 * (dp3 - over_interests(p3 * dp3))
        spread(dl3, 4)
        dc2 = by_interest(bilt_ref, weighted_sum(b, 4))
        ds2 = squash_back(s2, dc2)
        v2 = keep_vec(by_interest(bil_ref, ds2), 1)
        dp2 = jnp.where(live, agreement(b, v2), 0.0)
        dl2 = dl3 + p2 * (dp2 - over_interests(p2 * dp2))
        spread(dl2, 3)
        dc1 = by_interest(bilt_ref, weighted_sum(b, 3))
        ds1 = squash_back(s1, dc1)
        keep_vec(by_interest(bil_ref, ds1), 0)
        for t in range(tile_count):
            rg_ref[t * lanes:(t + 1) * lanes, :] = dot(mcat[t * lanes:(t + 1) * lanes, :], vcat[...]).astype(bf16)

        def slot_chunk(i, carry):
            for t in range(tile_count):
                tile = b * tile_count + t
                lo3 = lo_ref[tile].reshape(cap // 16, 16, lanes)
                orow16 = jnp.broadcast_to(owner_ref[pl.ds(tile, 1), :], (16, lanes))
                for oo in range(256 // cap):
                    ind = indicator(orow16, i * (256 // cap) + oo)
                    oh_rows[oo * cap:(oo + 1) * cap, t * lanes:(t + 1) * lanes] = (
                        lo3 * ind[None]).reshape(cap, lanes)
            start = pl.multiple_of(i * 256, 256)
            slot_acc[pl.ds(start, 256), :] += dot(oh_rows[...], rg_ref[...])
            return carry

        lax.fori_loop(0, slots // 256, slot_chunk, 0)
        return carry

    lax.fori_loop(0, block_count, per_block, 0)
    slotgrad_ref[...] = slot_acc[...].astype(bf16)


def route(fetched, bilinear, history, lengths, init_logits, interest_grad, cap):
    slots, width = fetched.shape
    users, hist_count = history.shape
    interests = init_logits.shape[2]
    blocks = users // BLOCK_USERS
    tile_count = -(-hist_count // TILE_POSITIONS)
    positions = tile_count * TILE_POSITIONS
    padded = -(-positions // 8) * 8
    lanes = interests * BLOCK_USERS
    hist_t = jnp.pad(history.T, ((0, positions - hist_count), (0, 0)))
    hist_t = hist_t.reshape(tile_count, TILE_POSITIONS, blocks, BLOCK_USERS).transpose(2, 0, 1, 3)
    hist_t = hist_t.reshape(blocks * tile_count, lanes)
    owner = hist_t // cap
    slot = hist_t % cap
    lens = jnp.broadcast_to(lengths.reshape(blocks, 1, BLOCK_USERS), (blocks, interests, BLOCK_USERS)).reshape(blocks, lanes)
    logits = init_logits.reshape(blocks, BLOCK_USERS, hist_count, interests).transpose(0, 2, 3, 1)
    logits = jnp.pad(logits.reshape(blocks, hist_count, lanes), ((0, 0), (0, padded - hist_count), (0, 0)))
    cot = interest_grad.reshape(blocks, BLOCK_USERS, interests, width).transpose(0, 3, 2, 1).reshape(blocks, width, lanes)
    bilt = bilinear.reshape(width, interests, width).transpose(2, 1, 0).reshape(width, interests * width)
    vmem = functools.partial(pltpu.VMEM)
    tiles = blocks * tile_count
    rows = tile_count * lanes
    out, slot_grads = pl.pallas_call(
        functools.partial(routing_kernel, interests, tile_count),
        out_shape=(
            jax.ShapeDtypeStruct((blocks, lanes, width), bf16),
            jax.ShapeDtypeStruct((slots, width), bf16),
        ),
        scratch_shapes=[
            pltpu.VMEM((width, slots), bf16),
            pltpu.VMEM((tiles, lanes, width), bf16),
            pltpu.VMEM((tiles, width, lanes), bf16),
            pltpu.VMEM((tiles, cap, lanes), bf16),
            pltpu.VMEM((slots, lanes), bf16),
            pltpu.VMEM((slots, lanes), bf16),
            pltpu.VMEM((rows, 5 * lanes), bf16),
            pltpu.VMEM((5 * lanes, width), bf16),
            pltpu.VMEM((interests * width, lanes), bf16),
            pltpu.VMEM((rows, width), bf16),
            pltpu.VMEM((256, rows), bf16),
            pltpu.VMEM((padded, lanes), f32),
            pltpu.VMEM((slots, width), f32),
        ],
        compiler_params=pltpu.CompilerParams(vmem_limit_bytes=60 * 1024 * 1024),
    )(fetched, bilinear, bilt, owner, slot, lens, logits, cot)
    capsules = out.reshape(blocks, interests, BLOCK_USERS, width).transpose(0, 2, 1, 3).reshape(users, interests, width)
    return capsules, slot_grads


def table_kernel(target_ref, rows_ref, out_ref, rows32, acc, sem):
    count = rows_ref.shape[0]
    table_rows = out_ref.shape[0]
    rows32[...] = rows_ref[...].astype(f32)
    acc[...] = jnp.zeros_like(acc)

    def step(i, carry):
        base = pl.multiple_of(i * 8, 8)
        where = [target_ref[base + j] for j in range(8)]
        sums = [acc[pl.ds(where[j], 1), :] + rows32[pl.ds(base + j, 1), :] for j in range(8)]
        for j in range(8):
            acc[pl.ds(where[j], 1), :] = sums[j]
        return carry

    lax.fori_loop(0, count // 8, step, 0)
    copy = pltpu.make_async_copy(acc.at[pl.ds(0, table_rows), :], out_ref, sem)
    copy.start()
    copy.wait()


def add_to_table(returned, wanted, table_rows):
    count, width = returned.shape
    spare = table_rows + lax.rem(lax.broadcasted_iota(jnp.int32, (count,), 0), 8)
    targets = jnp.where(wanted >= 0, wanted, spare)
    return pl.pallas_call(
        table_kernel,
        out_shape=jax.ShapeDtypeStruct((table_rows, width), f32),
        in_specs=[
            pl.BlockSpec(memory_space=pltpu.SMEM),
            pl.BlockSpec(memory_space=pltpu.VMEM),
        ],
        out_specs=pl.BlockSpec(memory_space=pl.ANY),
        scratch_shapes=[
            pltpu.VMEM((count, width), f32),
            pltpu.VMEM((table_rows + 8, width), f32),
            pltpu.SemaphoreType.DMA,
        ],
        compiler_params=pltpu.CompilerParams(vmem_limit_bytes=60 * 1024 * 1024),
    )(targets, returned)


def exchange(x):
    return lax.all_to_all(x, AXES, split_axis=0, concat_axis=0, tiled=True)


def local(item_table, bilinear, requests, history, lengths, init_logits, interest_grad):
    asked_ids = requests[0]
    owner_count, slot_count = asked_ids.shape
    local_table_rows, width = item_table.shape
    wanted = exchange(asked_ids)
    found = item_table.at[jnp.maximum(wanted, 0).reshape(-1)].get(mode="promise_in_bounds")
    fetched = exchange(found.reshape(owner_count, slot_count, width)).reshape(owner_count * slot_count, width)
    capsules, slot_grads = route(fetched, bilinear, history, lengths, init_logits, interest_grad, slot_count)
    returned = exchange(slot_grads.reshape(owner_count, slot_count, width)).reshape(owner_count * slot_count, width)
    table_grad = add_to_table(returned, wanted.reshape(-1), local_table_rows)
    return capsules, table_grad


def solution(mesh):
    placed = (
        P(AXES, None),
        P(),
        P(AXES, None, None),
        P(AXES, None),
        P(AXES),
        P(AXES, None, None),
        P(AXES, None, None),
    )
    return jax.shard_map(
        local,
        mesh=mesh,
        in_specs=placed,
        out_specs=(P(AXES, None, None), P(AXES, None)),
        check_vma=False,
    )
```

time: 612 us -> 201 us (0.33); the launches traced: 600 us -> 200 us
  other arithmetic: 210 us -> 2.04 us
  local copies, waits for them, and re-layouts: 176 us -> 23 us
  matrix products: 152 us -> 0 us
  Pallas kernels: 0 us -> 112 us
  blocking collectives: 44 us -> 14.4 us
  waiting for transfers between devices: 14.8 us -> 41.8 us
    dot_general x11 -> x0, matrix products: 152 us -> none  [the longest x5 67.3 us: route_interests(): jnp.einsum('rmq,rmqs->rqs', coupling_weight.astype(jnp.bfloat16), remappe...]
    pallas_call x0 -> x2, Pallas kernels: none -> 112 us  [the longest x1 98.8 us: route(): pl.pallas_call(functools.partial(routing_kernel, interests, tile_count),...]
    add_any x8 -> x0, other arithmetic: 86.9 us -> none  [the longest x1 77.3 us: route_interests(): jnp.einsum('rmq,rmqs->rqs', coupling_weight.astype(jnp.bfloat16), remappe...]
    scatter-add x2 -> x0, other arithmetic: 85.3 us -> none  [the longest x1 69.6 us: local(): jax.ops.segment_sum(row_grad.reshape(-1, feature_width).astype(jnp.float3...]
    reshape x3 -> x12, local copies, waits for them, and re-layouts: 43.3 us -> 4.95 us  [the longest x1 1.37 us: route(): interest_grad.reshape(blocks, BLOCK_USERS, interests, width)]
    gather x2 -> x1, local copies, waits for them, and re-layouts: 45.3 us -> 11.3 us  [local(): item_table.at[jnp.maximum(wanted, 0).reshape(-1)]]
    all_to_all x2 -> x1, blocking collectives: 44 us -> 14.4 us  [exchange(): return lax.all_to_all(x, AXES, split_axis=0, concat_axis=0, tiled=True)]
    all_to_all x1 -> x2, waiting for transfers between devices: 14.8 us -> 41.8 us  [exchange(): return lax.all_to_all(x, AXES, split_axis=0, concat_axis=0, tiled=True)]
  transfers between devices with their start and end apart: 1 -> 2, of which waited for: 1 -> 2; matrix products, arithmetic and copies ran while one was open for 2% -> 5% of each run, Pallas kernels for 0% -> 0%
where the time goes in v1:
time: 201 us; the launch traced here: 200 us
  Pallas kernels  112 us (56%)
  waiting for transfers between devices  41.8 us (21%)
  local copies, waits for them, and re-layouts  23 us (11%)
  blocking collectives  14.4 us (7%)
  starting transfers between devices  6.32 us (3%)
  other arithmetic  2.04 us (1%)
    pallas_call x1, Pallas kernels, route(): pl.pallas_call(functools.partial(routing_kernel, interests, tile_count),...  98.8 us
    all_to_all x2, waiting for transfers between devices, exchange(): return lax.all_to_all(x, AXES, split_axis=0, concat_axis=0, tiled=True)  41.8 us
    all_to_all x1, blocking collectives, exchange(): return lax.all_to_all(x, AXES, split_axis=0, concat_axis=0, tiled=True)  14.4 us
    pallas_call x1, Pallas kernels, add_to_table(): pl.pallas_call(table_kernel, out_shape=jax.ShapeDtypeStruct((table_rows,...  13.1 us
    gather x1, local copies, waits for them, and re-layouts, local(): item_table.at[jnp.maximum(wanted, 0).reshape(-1)]  11.3 us
    all_to_all x2, starting transfers between devices, exchange(): return lax.all_to_all(x, AXES, split_axis=0, concat_axis=0, tiled=True)  6.32 us
  transfers between devices with their start and end apart: 2, of which 2 were waited for; matrix products, arithmetic and copies ran while one was open for 5% of the time, Pallas kernels for 0%

profile of v1, /device:TPU:0, one launch (start us, length us, event | category | flops | bytes accessed | tf_op | source)
XLA Modules:
  0.0 200.5 jit_solution(808810551185490822)
XLA Ops:
  0.6 14.4 %all_to_all.19 = s32[32,1,64]{2,1,0:T(1,128)S(1)} all-to-all(s32[32,1,64]{2,1,0:T(1,128)} %bitcast.39), channel_id=1, replica_groups=mesh['gx'=4,'gy'=8] {'gx','gy'}, dimensions={0} | all-to-all | bytes 16384 | tf_op jit(solution)/shard_map/all_to_all | solution.py:287
  15.1 0.5 broadcast.54
  15.6 0.7 fusion.2
  16.4 11.3 %gather_fusion = bf16[2048,256]{1,0:T(8,128)(2,1)} fusion(bf16[8192,256]{1,0:T(8,128)(2,1)} %param.7, s32[2048]{0:T(1024)S(1)} %broadcast_clamp_fusion), kind=kCustom, calls=%fused_computation | custom fusion | bytes 2105344 | tf_op jit(solution)/shard_map/gather | solution.py:295
  27.7 2.8 %all-to-all-start.1 = ((bf16[32,64,256]{2,1,0:T(8,128)(2,1)}), bf16[32,64,256]{2,1,0:T(8,128)(2,1)S(1)}, u32[]{:S(2)}, u32[]{:S(2)}) async-start(bf16[32,64,256]{2,1,0:T(8,128)(2,1)} %bitcast.1), calls=%async_computation.1 | async-start | bytes 2097152 | tf_op jit(solution)/shard_map/all_to_all | solution.py:287
  30.6 0.7 reshape.78.lens_ref
  31.5 1.2 reshape.79
  32.8 0.3 reshape.80
  33.1 0.4 reshape.74
  33.5 0.6 copy.28
  34.1 0.9 copy.36
  35.0 0.2 copy.32
  35.3 1.4 copy.34.cot_ref
  36.7 0.7 pad.9.logit_ref
  37.4 0.7 add_select_fusion
  38.1 18.5 %all-to-all-done.1 = bf16[32,64,256]{2,1,0:T(8,128)(2,1)S(1)} async-done(((bf16[32,64,256]{2,1,0:T(8,128)(2,1)}), bf16[32,64,256]{2,1,0:T(8,128)(2,1)S(1)}, u32[]{:S(2)}, u32[]{:S(2)}) %all-to-all-start.1) | async-done | bytes 1048608 | tf_op jit(solution)/shard_map/all_to_all | solution.py:287
  56.6 1.0 copy-done
  57.6 98.8 %shard_map.86 = (bf16[4,256,256]{2,1,0:T(8,128)(2,1)}, bf16[2048,256]{1,0:T(8,128)(2,1)}) custom-call(bf16[2048,256]{1,0:T(8,128)(2,1)} %bitcast.29, bf16[256,1024]{1,0:T(8,128)(2,1)} %bil_ref.1, bf16[256,1024]{1,0:T(8,128)(2,1)} %bitcast.32, s32[52,256]{1,0:T(8,128)} %get-tuple-element.9.owner_ref, s32[52,256]{1,0:T(8,128)} %get-tuple-element.8.slot_ref, ...), custom_call_target="tpu_custom_call" | custom-call | tf_op jit(solution)/shard_map/pallas_call | solution.py:218
  156.5 3.5 %all-to-all-start.2 = ((bf16[32,64,256]{2,1,0:T(8,128)(2,1)}), bf16[32,64,256]{2,1,0:T(8,128)(2,1)S(1)}, u32[]{:S(2)}, u32[]{:S(2)}) async-start(bf16[32,64,256]{2,1,0:T(8,128)(2,1)} %bitcast.34), calls=%async_computation.2 | async-start | bytes 2097152 | tf_op jit(solution)/shard_map/all_to_all | solution.py:287
  160.1 0.6 compare_select_fusion.target_ref
  160.7 2.2 %copy.35 = bf16[4,64,4,256]{3,2,1,0:T(4,128)(2,1)} copy(bf16[4,64,4,256]{3,1,2,0:T(8,128)(2,1)} %bitcast.35) | data formatting | bytes 1048576 | tf_op jit(solution)/shard_map/transpose | solution.py:241
  162.9 23.3 %all-to-all-done.2 = bf16[32,64,256]{2,1,0:T(8,128)(2,1)S(1)} async-done(((bf16[32,64,256]{2,1,0:T(8,128)(2,1)}), bf16[32,64,256]{2,1,0:T(8,128)(2,1)S(1)}, u32[]{:S(2)}, u32[]{:S(2)}) %all-to-all-start.2) | async-done | bytes 1048608 | tf_op jit(solution)/shard_map/all_to_all | solution.py:287
  186.2 1.0 copy-done.1
  187.2 13.1 %shard_map.87 = f32[8192,256]{1,0:T(8,128)} custom-call(s32[2048]{0:T(1024)} %compare_select_fusion.target_ref, bf16[2048,256]{1,0:T(8,128)(2,1)} %bitcast.30), custom_call_target="tpu_custom_call" | custom-call | tf_op jit(solution)/shard_map/pallas_call | solution.py:269
  (22 shorter events, 0.7 us)
Async XLA Ops:
  16.4 14.0 %copy-start.5 = (s32[256]{0:T(256)S(1)}, s32[256]{0:T(256)}, u32[]{:S(2)}) copy-start(s32[256]{0:T(256)} %param.11) | copy-start | bytes 3076
  16.4 14.8 %copy-start.4 = (s32[256,50]{0,1:T(8,128)S(1)}, s32[256,50]{0,1:T(8,128)}, u32[]{:S(2)}) copy-start(s32[256,50]{0,1:T(8,128)} %param.10) | copy-start | bytes 153604
  27.7 5.4 %copy-start.2 = (bf16[256,1024]{1,0:T(8,128)(2,1)S(1)}, bf16[256,1024]{1,0:T(8,128)(2,1)}, u32[]{:S(2)}) copy-start(bf16[256,1024]{1,0:T(8,128)(2,1)} %bil_ref.1) | copy-start | bytes 1572868
  27.7 7.4 %copy-start.3 = (f32[256,4,256]{2,1,0:T(4,128)S(1)}, f32[256,4,256]{2,1,0:T(4,128)}, u32[]{:S(2)}) copy-start(f32[256,4,256]{2,1,0:T(4,128)} %param.13) | copy-start | bytes 3145732
  27.7 29.0 %all-to-all-start.1 = ((bf16[32,64,256]{2,1,0:T(8,128)(2,1)}), bf16[32,64,256]{2,1,0:T(8,128)(2,1)S(1)}, u32[]{:S(2)}, u32[]{:S(2)}) async-start(bf16[32,64,256]{2,1,0:T(8,128)(2,1)} %bitcast.1), calls=%async_computation.1 | async-start | bytes 2097152 | tf_op jit(solution)/shard_map/all_to_all | solution.py:287
  56.6 1.0 copy-start
  156.5 29.8 %all-to-all-start.2 = ((bf16[32,64,256]{2,1,0:T(8,128)(2,1)}), bf16[32,64,256]{2,1,0:T(8,128)(2,1)S(1)}, u32[]{:S(2)}, u32[]{:S(2)}) async-start(bf16[32,64,256]{2,1,0:T(8,128)(2,1)} %bitcast.34), calls=%async_computation.2 | async-start | bytes 2097152 | tf_op jit(solution)/shard_map/all_to_all | solution.py:287
  186.2 1.0 copy-start.1

commit v2 on v1

v2 whole, which is shorter than its diff:
```python
import functools

import jax
import jax.numpy as jnp
from jax import lax
from jax.experimental import pallas as pl
from jax.experimental.pallas import tpu as pltpu
from jax.sharding import PartitionSpec as P

ITERS = 3
squash_eps = 1e-06
AXES = ("gx", "gy")
BLOCK_USERS = 64
TILE_POSITIONS = 4
GROUP_USERS = 16
GROUP_ROWS = 8
COPIES = 8
VARIANTS = (8,)
f32 = jnp.float32
bf16 = jnp.bfloat16


def dot(a, b):
    return jnp.dot(a, b, preferred_element_type=f32)


def routing_kernel(
    interest_count, variants,
    need_ref, fetched_ref, bil_ref, bilt_ref, owner_ref, slot_ref, lens_ref, logit_ref, cot_ref,
    interests_ref, slotgrad_ref,
    fetched_t, gram, x_ref, xt_ref, lo_ref, oht_a, oht_b, mix, vcat, stack, rg_ref, oh_rows,
    rows_a, coefs, coef_rows, mix_g, z_ref, slot_acc,
):
    slots, width = fetched_ref.shape
    blocks, tiles, lanes = owner_ref.shape
    cap = lo_ref.shape[1]
    owners = slots // cap
    users = lanes // interest_count
    groups = users // GROUP_USERS
    group_lanes = lanes // groups
    chunk = oh_rows.shape[0]
    padded = logit_ref.shape[1]

    for c in range(0, slots, 256):
        fetched_t[:, c:c + 256] = fetched_ref[c:c + 256, :].T
    for k in range(interest_count):
        part = bil_ref[:, k * width:(k + 1) * width]
        gram[:, k * width:(k + 1) * width] = lax.dot_general(
            part, part, (((1,), (1,)), ((), ())), preferred_element_type=f32).astype(bf16)
    slot_acc[...] = jnp.zeros_like(slot_acc)
    vcat[...] = jnp.zeros_like(vcat)

    slot_iota = lax.broadcasted_iota(jnp.int32, (cap, lanes), 0)

    def col_user(lane):
        return (lane // group_lanes) * GROUP_USERS + lane % GROUP_USERS

    diag = col_user(lax.broadcasted_iota(jnp.int32, (users, lanes), 1)) == lax.broadcasted_iota(jnp.int32, (users, lanes), 0)
    lane_k = (lax.broadcasted_iota(jnp.int32, (width, lanes), 1) // GROUP_USERS) % interest_count
    half_lane = lax.broadcasted_iota(jnp.int32, (padded, 128), 1)
    mix_lanes = mix_g.shape[1]
    diag_g = (lax.broadcasted_iota(jnp.int32, (GROUP_USERS, mix_lanes), 1) % GROUP_USERS
              == lax.broadcasted_iota(jnp.int32, (GROUP_USERS, mix_lanes), 0))
    pos_iota = lax.broadcasted_iota(jnp.int32, (padded, lanes), 0)

    def indicator(orow16, o):
        return jnp.where(orow16 == o, 1.0, 0.0).astype(bf16)

    def over_interests(v):
        parts = []
        for h in range(0, lanes, 128):
            s = v[:, h:h + 128]
            step = group_lanes // 2
            while step >= GROUP_USERS:
                low = half_lane % (2 * step) < step
                s = s + jnp.where(low, pltpu.roll(s, 128 - step, 1), pltpu.roll(s, step, 1))
                step //= 2
            parts.append(s)
        return jnp.concatenate(parts, axis=1)

    def softmax(v):
        e = jnp.exp(v)
        return e / over_interests(e)

    def by_interest(mat_ref, v):
        zero = jnp.zeros_like(v)
        for k in range(interest_count):
            stack[k * width:(k + 1) * width, :] = jnp.where(lane_k == k, v, zero).astype(bf16)
        return dot(mat_ref[...], stack[...])

    def squash_parts(n):
        root = jnp.sqrt(n + squash_eps)
        fac = root / (1.0 + n)
        slope = (0.5 * (1.0 + n) / root - root) / ((1.0 + n) * (1.0 + n))
        return fac, 2.0 * slope

    def keep_vec(vec_t, j):
        vb = vec_t.astype(bf16)
        vn = vb.T
        for g in range(groups):
            vcat[g, j * group_lanes:(j + 1) * group_lanes, :] = vn[g * group_lanes:(g + 1) * group_lanes, :]
        return vb

    def block_body(b, tile_count):
        positions = tile_count * TILE_POSITIONS

        def build(t, buf):
            crow = slot_ref[b, pl.ds(t, 1), :]
            orow16 = jnp.broadcast_to(owner_ref[b, pl.ds(t, 1), :], (16, lanes))
            lo = jnp.where(slot_iota == crow, 1.0, 0.0).astype(bf16)
            lo_ref[t] = lo
            lo3 = lo.reshape(cap // 16, 16, lanes)
            for o in range(owners):
                buf[o * cap:(o + 1) * cap, :] = (lo3 * indicator(orow16, o)[None]).reshape(cap, lanes)

        def gather(t, buf):
            xtb = dot(fetched_t[...], buf[...]).astype(bf16)
            xt_ref[t] = xtb
            x_ref[t] = xtb.T

        build(0, oht_a)

        def gather_pair(i, carry):
            t = 2 * i
            build(t + 1, oht_b)
            gather(t, oht_a)
            build(jnp.minimum(t + 2, tile_count - 1), oht_a)
            gather(t + 1, oht_b)
            return carry

        lax.fori_loop(0, tile_count // 2, gather_pair, 0)
        if tile_count % 2:
            gather(tile_count - 1, oht_a)

        def weighted_sum(coef, j):
            coefs[j] = coef
            for l in range(positions):
                row = jnp.broadcast_to(coefs[j, l:l + 1, :], (users, lanes))
                mix[l * users:(l + 1) * users, :] = jnp.where(diag, row, 0.0).astype(bf16)
            total = jnp.zeros((width, lanes), f32)
            for t in range(tile_count):
                total = total + dot(xt_ref[t], mix[t * lanes:(t + 1) * lanes, :])
            return total

        def agreement(vec):
            for t in range(tile_count):
                prod = dot(x_ref[t], vec)
                for p in range(TILE_POSITIONS):
                    part = jnp.where(diag, prod[p * users:(p + 1) * users, :], 0.0)
                    l = t * TILE_POSITIONS + p
                    rows_a[l:l + 1, :] = jnp.sum(part, axis=0, keepdims=True)
            return jnp.where(live, rows_a[...], 0.0)

        live = pos_iota < lens_ref[pl.ds(b, 1), :]
        zero = jnp.zeros((padded, lanes), f32)

        def turn(p, j):
            xs = weighted_sum(jnp.where(live, p, zero), j)
            z = by_interest(gram, xs)
            n = jnp.maximum(jnp.sum(xs * z, axis=0, keepdims=True), 0.0)
            fac, slope = squash_parts(n)
            z_ref[j] = z
            return fac, slope, keep_vec(z * fac, 3 + j)

        logit1 = logit_ref[b]
        p1 = softmax(logit1)
        fac1, slope1, u1 = turn(p1, 0)
        logit2 = logit1 + agreement(u1)
        p2 = softmax(logit2)
        fac2, slope2, u2 = turn(p2, 1)
        logit3 = logit2 + agreement(u2)
        p3 = softmax(logit3)
        s3 = by_interest(bilt_ref, weighted_sum(jnp.where(live, p3, zero), 2))
        fac3, slope3 = squash_parts(jnp.sum(s3 * s3, axis=0, keepdims=True))
        interests_ref[b] = (s3 * fac3).astype(bf16).T
        dc3 = cot_ref[b]
        ds3 = dc3 * fac3 + s3 * (slope3 * jnp.sum(dc3 * s3, axis=0, keepdims=True))
        v3 = keep_vec(by_interest(bil_ref, ds3), 2)

        def turn_back(p, dp, later, j_vec, j_coef, fac, slope):
            dl = jnp.where(live, later + p * (dp - over_interests(p * dp)), zero)
            dxs = weighted_sum(dl, j_coef)
            y = by_interest(gram, dxs)
            z = z_ref[j_vec]
            inner = slope * jnp.sum(dxs * z, axis=0, keepdims=True)
            return dl, keep_vec(y * fac + z * inner, j_vec)

        dl3, v2 = turn_back(p3, agreement(v3), zero, 1, 4, fac2, slope2)
        turn_back(p2, agreement(v2), dl3, 0, 3, fac1, slope1)

        for g in range(groups):
            src = (g * group_lanes) // 128 * 128
            odd = (g * group_lanes) % 128

            def piece(j, dest):
                x = coefs[j, :, src:src + 128]
                return x if odd == dest else pltpu.roll(x, 64, 1)

            for q in range(0, 5, 2):
                low = piece(q, 0)
                high = piece(q + 1, 64) if q + 1 < 5 else jnp.zeros((padded, 128), f32)
                coef_rows[:, q * 64:q * 64 + 128] = jnp.where(half_lane < 64, low, high)
            for l in range(positions):
                row = jnp.broadcast_to(coef_rows[l:l + 1, :], (GROUP_USERS, mix_lanes))
                mix_g[l * GROUP_USERS:(l + 1) * GROUP_USERS, :] = jnp.where(diag_g, row, 0.0).astype(bf16)
            grads = dot(mix_g[0:positions * GROUP_USERS, :], vcat[g]).astype(bf16)
            for l in range(positions):
                start = l * users + g * GROUP_USERS
                rg_ref[start:start + GROUP_USERS, :] = grads[l * GROUP_USERS:(l + 1) * GROUP_USERS, :]

        def slot_chunk(i, carry):
            for t in range(tile_count):
                lo3 = lo_ref[t].reshape(cap // 16, 16, lanes)
                orow16 = jnp.broadcast_to(owner_ref[b, t:t + 1, :], (16, lanes))
                for oo in range(chunk // cap):
                    ind = indicator(orow16, i * (chunk // cap) + oo)
                    oh_rows[oo * cap:(oo + 1) * cap, t * lanes:(t + 1) * lanes] = (
                        lo3 * ind[None]).reshape(cap, lanes)
            start = pl.multiple_of(i * chunk, chunk)
            rows = tile_count * lanes
            slot_acc[pl.ds(start, chunk), :] += dot(oh_rows[:, 0:rows], rg_ref[0:rows, :])
            return carry

        lax.fori_loop(0, slots // chunk, slot_chunk, 0)

    def per_block(b, carry):
        need = need_ref[b]
        for i, count in enumerate(variants):
            fits = need <= count
            if i + 1 < len(variants):
                fits = jnp.logical_and(fits, need > variants[i + 1])

            @pl.when(fits)
            def _():
                block_body(b, count)

        return carry

    lax.fori_loop(0, blocks, per_block, 0)
    slotgrad_ref[...] = slot_acc[...].astype(bf16)


def prepare(history, lengths, init_logits, interest_grad, cap):
    users, hist_count = history.shape
    interests = init_logits.shape[2]
    width = interest_grad.shape[2]
    lanes = interests * BLOCK_USERS
    blocks = users // BLOCK_USERS
    tile_count = -(-hist_count // TILE_POSITIONS)
    positions = tile_count * TILE_POSITIONS
    padded = -(-positions // 8) * 8
    index = lax.iota(jnp.int32, users)
    ahead = (lengths[None, :] > lengths[:, None]) | (
        (lengths[None, :] == lengths[:, None]) & (index[None, :] < index[:, None]))
    rank = jnp.sum(ahead.astype(jnp.int32), axis=1)
    order = (rank[:, None] == index[None, :]).astype(bf16)
    column = lax.iota(jnp.int32, users * interests)
    block, rest = column // lanes, column % lanes
    group_lanes = interests * GROUP_USERS
    user = block * BLOCK_USERS + rest // group_lanes * GROUP_USERS + rest % GROUP_USERS
    interest = rest // GROUP_USERS % interests
    select = ((rank[:, None, None] == user[None, None, :])
              & (lax.iota(jnp.int32, interests)[None, :, None] == interest[None, None, :]))
    select = select.reshape(users * interests, users * interests)
    by_k = ((rank[None, :, None] == user[None, None, :])
            & (lax.iota(jnp.int32, interests)[:, None, None] == interest[None, None, :]))
    by_k = by_k.reshape(users * interests, users * interests)

    def sort_positions(values):
        s = jnp.dot(values.astype(bf16).T, order, preferred_element_type=f32).astype(jnp.int32)
        s = jnp.pad(s, ((0, positions - hist_count), (0, 0)))
        s = s.reshape(tile_count, TILE_POSITIONS, blocks, BLOCK_USERS).transpose(2, 0, 1, 3)
        return s.reshape(blocks, tile_count, TILE_POSITIONS * BLOCK_USERS)

    owner = sort_positions(history // cap)
    slot = sort_positions(history % cap)
    sorted_lens = jnp.sum(jnp.where(rank[:, None] == index[None, :], lengths[:, None], 0), axis=0)
    need = (sorted_lens[::BLOCK_USERS] + TILE_POSITIONS - 1) // TILE_POSITIONS
    lens = jnp.sum(jnp.where(rank[:, None] == user[None, :], lengths[:, None], 0), axis=0).reshape(blocks, lanes)
    flat = init_logits.transpose(1, 2, 0).reshape(hist_count, interests * users)
    logits = jnp.dot(flat, by_k.astype(f32), precision=lax.Precision.HIGHEST, preferred_element_type=f32)
    logits = jnp.pad(logits, ((0, padded - hist_count), (0, 0))).reshape(padded, blocks, lanes).transpose(1, 0, 2)
    grads = interest_grad.reshape(users * interests, width)
    cot = lax.dot_general(grads.astype(bf16), select.astype(bf16), (((0,), (0,)), ((), ())), preferred_element_type=f32)
    cot = cot.reshape(width, blocks, lanes).transpose(1, 0, 2)
    return owner, slot, need, lens, logits, cot, select


def route(fetched, bilinear, prepared, cap):
    owner, slot, need, lens, logits, cot, select = prepared
    slots, width = fetched.shape
    blocks, tile_count, lanes = owner.shape
    padded = logits.shape[1]
    interests = bilinear.shape[1] // width
    users = lanes // interests
    groups = users // GROUP_USERS
    mix_lanes = -(-5 * lanes // groups // 128) * 128
    bilt = bilinear.reshape(width, interests, width).transpose(2, 1, 0).reshape(width, interests * width)
    rows = tile_count * lanes
    variants = [tile_count] + [v for v in VARIANTS if v < tile_count]
    chunk = 512
    out, slot_grads = pl.pallas_call(
        functools.partial(routing_kernel, interests, variants),
        out_shape=(
            jax.ShapeDtypeStruct((blocks, lanes, width), bf16),
            jax.ShapeDtypeStruct((slots, width), bf16),
        ),
        in_specs=[pl.BlockSpec(memory_space=pltpu.SMEM)] + [pl.BlockSpec(memory_space=pltpu.VMEM)] * 8,
        scratch_shapes=[
            pltpu.VMEM((width, slots), bf16),
            pltpu.VMEM((width, interests * width), bf16),
            pltpu.VMEM((tile_count, lanes, width), bf16),
            pltpu.VMEM((tile_count, width, lanes), bf16),
            pltpu.VMEM((tile_count, cap, lanes), bf16),
            pltpu.VMEM((slots, lanes), bf16),
            pltpu.VMEM((slots, lanes), bf16),
            pltpu.VMEM((rows, lanes), bf16),
            pltpu.VMEM((groups, mix_lanes, width), bf16),
            pltpu.VMEM((interests * width, lanes), bf16),
            pltpu.VMEM((rows, width), bf16),
            pltpu.VMEM((chunk, rows), bf16),
            pltpu.VMEM((padded, lanes), f32),
            pltpu.VMEM((5, padded, lanes), f32),
            pltpu.VMEM((padded, mix_lanes), f32),
            pltpu.VMEM((rows // groups, mix_lanes), bf16),
            pltpu.VMEM((2, width, lanes), f32),
            pltpu.VMEM((slots, width), f32),
        ],
        compiler_params=pltpu.CompilerParams(vmem_limit_bytes=60 * 1024 * 1024),
    )(need, fetched, bilinear, bilt, owner, slot, lens, logits, cot)
    capsules = jnp.dot(select.astype(bf16), out.reshape(blocks * lanes, width), preferred_element_type=f32)
    return capsules.astype(bf16).reshape(blocks * users, interests, width), slot_grads


def fetch_kernel(wanted_ref, table_ref, out_ref, staged, table32, rows32, sems):
    parts = sems.shape[0]
    part = table_ref.shape[0] // parts
    copies = [
        pltpu.make_async_copy(table_ref.at[pl.ds(p * part, part), :], staged.at[pl.ds(p * part, part), :], sems.at[p])
        for p in range(parts)
    ]
    for copy in copies:
        copy.start()
    for p in range(parts):
        copies[p].wait()

        def widen(i, carry):
            base = pl.multiple_of(p * part + i * 128, 128)
            table32[pl.ds(base, 128), :] = staged[pl.ds(base, 128), :].astype(f32)
            return carry

        lax.fori_loop(0, part // 128, widen, 0)

    def copy_rows(i, carry):
        base = pl.multiple_of(i * 8, 8)
        rows = [table32[pl.ds(wanted_ref[base + j], 1), :] for j in range(8)]
        rows32[pl.ds(base, 8), :] = jnp.concatenate(rows, axis=0)
        return carry

    lax.fori_loop(0, out_ref.shape[0] // 8, copy_rows, 0, unroll=2)
    out_ref[...] = rows32[...].astype(bf16)


def fetch_rows(table, wanted):
    table_rows, width = table.shape
    count = wanted.shape[0]
    return pl.pallas_call(
        fetch_kernel,
        out_shape=jax.ShapeDtypeStruct((count, width), bf16),
        in_specs=[pl.BlockSpec(memory_space=pltpu.SMEM), pl.BlockSpec(memory_space=pl.ANY)],
        scratch_shapes=[
            pltpu.VMEM((table_rows, width), bf16),
            pltpu.VMEM((table_rows, width), f32),
            pltpu.VMEM((count, width), f32),
            pltpu.SemaphoreType.DMA((COPIES,)),
        ],
        compiler_params=pltpu.CompilerParams(vmem_limit_bytes=60 * 1024 * 1024),
    )(wanted, table)


def table_kernel(target_ref, rows_ref, out_ref, acc, sems):
    count = rows_ref.shape[0]
    parts = sems.shape[0]
    part = out_ref.shape[0] // parts
    acc[...] = jnp.zeros_like(acc)

    def step(i, carry):
        base = pl.multiple_of(i * 16, 16)
        rows = rows_ref[pl.ds(base, 16), :].astype(f32)
        where = [target_ref[base + j] for j in range(16)]
        for q in range(0, 16, GROUP_ROWS):
            sums = [acc[pl.ds(where[j], 1), :] + rows[j:j + 1, :] for j in range(q, q + GROUP_ROWS)]
            for j in range(q, q + GROUP_ROWS):
                acc[pl.ds(where[j], 1), :] = sums[j - q]
        return carry

    lax.fori_loop(0, count // 16, step, 0, unroll=2)
    copies = [
        pltpu.make_async_copy(acc.at[pl.ds(p * part, part), :], out_ref.at[pl.ds(p * part, part), :], sems.at[p])
        for p in range(parts)
    ]
    for copy in copies:
        copy.start()
    for copy in copies:
        copy.wait()


def add_to_table(returned, wanted, table_rows):
    count, width = returned.shape
    spare = table_rows + lax.rem(lax.broadcasted_iota(jnp.int32, (count,), 0), GROUP_ROWS)
    targets = jnp.where(wanted >= 0, wanted, spare)
    return pl.pallas_call(
        table_kernel,
        out_shape=jax.ShapeDtypeStruct((table_rows, width), f32),
        in_specs=[pl.BlockSpec(memory_space=pltpu.SMEM), pl.BlockSpec(memory_space=pltpu.VMEM)],
        out_specs=pl.BlockSpec(memory_space=pl.ANY),
        scratch_shapes=[
            pltpu.VMEM((table_rows + GROUP_ROWS, width), f32),
            pltpu.SemaphoreType.DMA((COPIES,)),
        ],
        compiler_params=pltpu.CompilerParams(vmem_limit_bytes=60 * 1024 * 1024),
    )(targets, returned)


def exchange(x):
    return lax.all_to_all(x, AXES, split_axis=0, concat_axis=0, tiled=True)


def local(item_table, bilinear, requests, history, lengths, init_logits, interest_grad):
    asked_ids = requests[0]
    owner_count, slot_count = asked_ids.shape
    local_table_rows, width = item_table.shape
    wanted = exchange(asked_ids)
    found = fetch_rows(item_table, jnp.maximum(wanted, 0).reshape(-1))
    fetched = exchange(found.reshape(owner_count, slot_count, width)).reshape(owner_count * slot_count, width)
    prepared = prepare(history, lengths, init_logits, interest_grad, slot_count)
    capsules, slot_grads = route(fetched, bilinear, prepared, slot_count)
    returned = exchange(slot_grads.reshape(owner_count, slot_count, width)).reshape(owner_count * slot_count, width)
    table_grad = add_to_table(returned, wanted.reshape(-1), local_table_rows)
    return capsules, table_grad


def solution(mesh):
    placed = (
        P(AXES, None),
        P(),
        P(AXES, None, None),
        P(AXES, None),
        P(AXES),
        P(AXES, None, None),
        P(AXES, None, None),
    )
    return jax.shard_map(
        local,
        mesh=mesh,
        in_specs=placed,
        out_specs=(P(AXES, None, None), P(AXES, None)),
        check_vma=False,
    )
```

time: 201 us -> 173 us (0.86)
  Pallas kernels: 112 us -> 93.1 us
  blocking collectives: 14.4 us -> 0 us
  starting transfers between devices: 6.32 us -> 16.7 us
  local copies, waits for them, and re-layouts: 23 us -> 13.2 us
  matrix products: 0 us -> 8.12 us
  waiting for transfers between devices: 41.8 us -> 34.9 us
  other arithmetic: 2.04 us -> 6.99 us
    pallas_call x1 -> x2, Pallas kernels: 98.8 us -> 83.7 us  [the longest x1 74.8 us: route(): pl.pallas_call(functools.partial(routing_kernel, interests, variants), ou...]
    all_to_all x1 -> x0, blocking collectives: 14.4 us -> none  [exchange(): return lax.all_to_all(x, AXES, split_axis=0, concat_axis=0, tiled=True)]
    gather x1 -> x0, local copies, waits for them, and re-layouts: 11.3 us -> none  [local(): item_table.at[jnp.maximum(wanted, 0).reshape(-1)]]
    all_to_all x2 -> x3, starting transfers between devices: 6.32 us -> 16.7 us  [exchange(): return lax.all_to_all(x, AXES, split_axis=0, concat_axis=0, tiled=True)]
    dot_general x0 -> x5, matrix products: none -> 8.12 us  [the longest x1 3.35 us: prepare(): lax.dot_general(grads.astype(bf16), select.astype(bf16), (((0,), (0,)), (...]
    all_to_all x2 -> x3, waiting for transfers between devices: 41.8 us -> 34.9 us  [exchange(): return lax.all_to_all(x, AXES, split_axis=0, concat_axis=0, tiled=True)]
    pallas_call x1, Pallas kernels: 13.1 us -> 9.45 us  [add_to_table(): pl.pallas_call(table_kernel, out_shape=jax.ShapeDtypeStruct((table_rows,...]
    reduce_sum x0 -> x3, other arithmetic: none -> 2.62 us  [the longest x1 0.94 us: prepare(): rank = jnp.sum(ahead.astype(jnp.int32), axis=1)]
  transfers between devices with their start and end apart: 2 -> 3, of which waited for: 2 -> 3; matrix products, arithmetic and copies ran while one was open for 5% -> 14% of each run, Pallas kernels for 0% -> 0%
where the time goes in v2:
time: 173 us; the launch traced here: 174 us
  Pallas kernels  93.1 us (54%)
  waiting for transfers between devices  34.9 us (20%)
  starting transfers between devices  16.7 us (10%)
  local copies, waits for them, and re-layouts  13.2 us (8%)
  matrix products  8.12 us (5%)
  other arithmetic  6.99 us (4%)
    pallas_call x1, Pallas kernels, route(): pl.pallas_call(functools.partial(routing_kernel, interests, variants), ou...  74.8 us
    all_to_all x3, waiting for transfers between devices, exchange(): return lax.all_to_all(x, AXES, split_axis=0, concat_axis=0, tiled=True)  34.9 us
    all_to_all x3, starting transfers between devices, exchange(): return lax.all_to_all(x, AXES, split_axis=0, concat_axis=0, tiled=True)  16.7 us
    pallas_call x1, Pallas kernels, add_to_table(): pl.pallas_call(table_kernel, out_shape=jax.ShapeDtypeStruct((table_rows,...  9.45 us
    pallas_call x1, Pallas kernels, fetch_rows(): pl.pallas_call(fetch_kernel, out_shape=jax.ShapeDtypeStruct((count, width...  8.82 us
  transfers between devices with their start and end apart: 3, of which 3 were waited for; matrix products, arithmetic and copies ran while one was open for 14% of the time, Pallas kernels for 0%

profile of v2, /device:TPU:0, one launch (start us, length us, event | category | flops | bytes accessed | tf_op | source)
XLA Modules:
  0.0 174.0 jit_solution(8179470313250124875)
XLA Ops:
  0.7 7.3 %all-to-all-start = ((s32[32,1,64]{2,1,0:T(1,128)}), s32[32,1,64]{2,1,0:T(1,128)S(1)}, u32[]{:S(2)}, u32[]{:S(2)}) async-start(s32[32,1,64]{2,1,0:T(1,128)} %bitcast.52), calls=%async_computation | async-start | bytes 32768 | tf_op jit(solution)/shard_map/all_to_all | solution.py:426
  8.0 0.9 convert_reduce_fusion
  9.0 0.8 select_reduce_fusion.1
  9.8 1.1 convolution_convert_fusion.1
  11.0 4.2 %all-to-all-done = s32[32,1,64]{2,1,0:T(1,128)S(1)} async-done(((s32[32,1,64]{2,1,0:T(1,128)}), s32[32,1,64]{2,1,0:T(1,128)S(1)}, u32[]{:S(2)}, u32[]{:S(2)}) %all-to-all-start) | async-done | bytes 8224 | tf_op jit(solution)/shard_map/all_to_all | solution.py:426
  17.0 8.8 %shard_map.86 = bf16[2048,256]{1,0:T(8,128)(2,1)} custom-call(s32[2048]{0:T(1024)} %get-tuple-element.7.wanted_ref, bf16[8192,256]{1,0:T(8,128)(2,1)} %table_ref.1), custom_call_target="tpu_custom_call" | custom-call | tf_op jit(solution)/shard_map/pallas_call | solution.py:367
  25.8 2.7 %all-to-all-start.1 = ((bf16[32,64,256]{2,1,0:T(8,128)(2,1)}), bf16[32,64,256]{2,1,0:T(8,128)(2,1)S(1)}, u32[]{:S(2)}, u32[]{:S(2)}) async-start(bf16[32,64,256]{2,1,0:T(8,128)(2,1)} %bitcast.41), calls=%async_computation.1 | async-start | bytes 2097152 | tf_op jit(solution)/shard_map/all_to_all | solution.py:426
  28.5 0.9 select_reduce_fusion
  32.3 1.4 fusion.6
  34.5 1.0 convert_element_type.33
  36.5 0.9 copy.46
  37.3 1.2 broadcast_and_fusion
  38.6 3.3 %fusion = f32[1024,256,1]{1,0,2:T(8,128)} fusion(pred[256,4,1024]{2,1,0:T(4,128)(4,1)S(1)} %broadcast_and_fusion, bf16[256,4,256]{2,1,0:T(4,128)(2,1)} %convert_element_type.33), kind=kOutput, calls=%fused_computation | convolution fusion | flops 536870912 | bytes 2621440 | tf_op jit(solution)/shard_map/dot_general | solution.py:284
  41.9 2.5 %copy.42 = f32[256,4,256]{2,0,1:T(8,128)} copy(f32[256,4,256]{0,2,1:T(8,128)} %bitcast.47) | data formatting | bytes 2097152 | tf_op jit(solution)/shard_map/reshape | solution.py:285
  45.1 9.6 %all-to-all-done.1 = bf16[32,64,256]{2,1,0:T(8,128)(2,1)S(1)} async-done(((bf16[32,64,256]{2,1,0:T(8,128)(2,1)}), bf16[32,64,256]{2,1,0:T(8,128)(2,1)S(1)}, u32[]{:S(2)}, u32[]{:S(2)}) %all-to-all-start.1) | async-done | bytes 1048608 | tf_op jit(solution)/shard_map/all_to_all | solution.py:426
  54.7 1.0 copy-done.1
  55.7 74.8 %shard_map.87 = (bf16[4,256,256]{2,1,0:T(8,128)(2,1)}, bf16[2048,256]{1,0:T(8,128)(2,1)}) custom-call(s32[4]{0:T(128)} %and_select_fusion.need_ref, bf16[2048,256]{1,0:T(8,128)(2,1)} %bitcast.40, bf16[256,1024]{1,0:T(8,128)(2,1)} %bil_ref.1, bf16[256,1024]{1,0:T(8,128)(2,1)} %bitcast.45, s32[4,13,256]{2,1,0:T(8,128)} %copy.43.owner_ref, ...), custom_call_target="tpu_custom_call" | custom-call | tf_op jit(solution)/shard_map/pallas_call | solution.py:302
  130.5 6.7 %all-to-all-start.2 = ((bf16[32,64,256]{2,1,0:T(8,128)(2,1)}), bf16[32,64,256]{2,1,0:T(8,128)(2,1)S(1)}, u32[]{:S(2)}, u32[]{:S(2)}) async-start(bf16[32,64,256]{2,1,0:T(8,128)(2,1)} %bitcast.46), calls=%async_computation.2 | async-start | bytes 2097152 | tf_op jit(solution)/shard_map/all_to_all | solution.py:426
  137.2 2.1 %and.182 = pred[1024,1024]{1,0:T(32,128)(4,1)} reshape(pred[256,4,1024]{2,1,0:T(4,128)(4,1)S(1)} %broadcast_and_fusion) | data formatting | bytes 2097152 | tf_op jit(solution)/shard_map/and | solution.py:262
  139.3 2.1 %convolution_convert_fusion = bf16[1024,256]{1,0:T(8,128)(2,1)S(1)} fusion(pred[1024,1024]{1,0:T(32,128)(4,1)} %and.182, bf16[1024,256]{1,0:T(8,128)(2,1)} %bitcast.53), kind=kOutput, calls=%fused_computation.7 | convolution fusion | flops 537133056 | bytes 2097152 | tf_op jit(solution)/shard_map/dot_general | solution.py:331
  141.4 0.9 reshape.318
  142.3 21.1 %all-to-all-done.2 = bf16[32,64,256]{2,1,0:T(8,128)(2,1)S(1)} async-done(((bf16[32,64,256]{2,1,0:T(8,128)(2,1)}), bf16[32,64,256]{2,1,0:T(8,128)(2,1)S(1)}, u32[]{:S(2)}, u32[]{:S(2)}) %all-to-all-start.2) | async-done | bytes 1048608 | tf_op jit(solution)/shard_map/all_to_all | solution.py:426
  163.4 1.0 copy-done.2
  164.4 9.4 %shard_map.88 = f32[8192,256]{1,0:T(8,128)} custom-call(s32[2048]{0:T(1024)} %get-tuple-element.6.target_ref, bf16[2048,256]{1,0:T(8,128)(2,1)} %bitcast.43), custom_call_target="tpu_custom_call" | custom-call | tf_op jit(solution)/shard_map/pallas_call | solution.py:412
  (36 shorter events, 7.2 us)
Async XLA Ops:
  0.6 31.6 %copy-start = (f32[256,50,4]{0,2,1:T(4,128)S(1)}, f32[256,50,4]{0,2,1:T(4,128)}, u32[]{:S(2)}) copy-start(f32[256,50,4]{0,2,1:T(4,128)} %param.12) | copy-start | bytes 614404
  0.6 30.2 %copy-start.5 = (s32[256,50]{0,1:T(8,128)S(1)}, s32[256,50]{0,1:T(8,128)}, u32[]{:S(2)}) copy-start(s32[256,50]{0,1:T(8,128)} %param.10) | copy-start | bytes 153604
  0.7 33.8 %copy-start.4 = (f32[256,4,256]{2,1,0:T(4,128)S(1)}, f32[256,4,256]{2,1,0:T(4,128)}, u32[]{:S(2)}) copy-start(f32[256,4,256]{2,1,0:T(4,128)} %param.13) | copy-start | bytes 3145732
  0.7 34.8 %copy-start.3 = (bf16[256,1024]{1,0:T(8,128)(2,1)S(1)}, bf16[256,1024]{1,0:T(8,128)(2,1)}, u32[]{:S(2)}) copy-start(bf16[256,1024]{1,0:T(8,128)(2,1)} %bil_ref.1) | copy-start | bytes 1572868
  0.7 14.4 %all-to-all-start = ((s32[32,1,64]{2,1,0:T(1,128)}), s32[32,1,64]{2,1,0:T(1,128)S(1)}, u32[]{:S(2)}, u32[]{:S(2)}) async-start(s32[32,1,64]{2,1,0:T(1,128)} %bitcast.52), calls=%async_computation | async-start | bytes 32768 | tf_op jit(solution)/shard_map/all_to_all | solution.py:426
  25.8 28.9 %all-to-all-start.1 = ((bf16[32,64,256]{2,1,0:T(8,128)(2,1)}), bf16[32,64,256]{2,1,0:T(8,128)(2,1)S(1)}, u32[]{:S(2)}, u32[]{:S(2)}) async-start(bf16[32,64,256]{2,1,0:T(8,128)(2,1)} %bitcast.41), calls=%async_computation.1 | async-start | bytes 2097152 | tf_op jit(solution)/shard_map/all_to_all | solution.py:426
  54.7 1.0 copy-start.1
  130.5 32.9 %all-to-all-start.2 = ((bf16[32,64,256]{2,1,0:T(8,128)(2,1)}), bf16[32,64,256]{2,1,0:T(8,128)(2,1)S(1)}, u32[]{:S(2)}, u32[]{:S(2)}) async-start(bf16[32,64,256]{2,1,0:T(8,128)(2,1)} %bitcast.46), calls=%async_computation.2 | async-start | bytes 2097152 | tf_op jit(solution)/shard_map/all_to_all | solution.py:426
  163.4 1.0 copy-start.2

commit v3 on v2

v3 whole, which is shorter than its diff:
```python
import functools

import jax
import jax.numpy as jnp
from jax import lax
from jax.experimental import pallas as pl
from jax.experimental.pallas import tpu as pltpu
from jax.sharding import PartitionSpec as P

ITERS = 3
squash_eps = 1e-06
AXES = ("gx", "gy")
BLOCK_USERS = 64
TILE_POSITIONS = 4
GROUP_USERS = 16
GROUP_ROWS = 8
COPIES = 8
OCTET = 8
PAIRS = 7
VMEM_BYTES = 60 * 1024 * 1024
f32 = jnp.float32
bf16 = jnp.bfloat16


def dot(a, b):
    return jnp.dot(a, b, preferred_element_type=f32)


def routing_kernel(
    interest_count,
    meta_ref, fetched_ref, bil_ref, bilt_ref, owner_ref, slot_ref, lens_ref, logit_ref, cot_ref,
    interests_ref, slotgrad_ref,
    fetched_t, gram, x_ref, xt_ref, lo_ref, oht_a, oht_b, mix, vecs, vcat, stack, oh_rows,
    sums, logit_now, p_ref, coefs, mix_g, z_ref, slot_acc,
):
    slots, width = fetched_ref.shape
    lanes = owner_ref.shape[2]
    blocks = interests_ref.shape[0]
    pair_max = xt_ref.shape[0]
    pair_rows = xt_ref.shape[2]
    cap = lo_ref.shape[1]
    owners = slots // cap
    users = lanes // interest_count
    groups = users // GROUP_USERS
    group_lanes = lanes // groups
    chunk = oh_rows.shape[0]
    mix_lanes = mix_g.shape[2]
    chunk_count = meta_ref[2 * pair_max]

    for c in range(0, slots, 256):
        fetched_t[:, c:c + 256] = fetched_ref[c:c + 256, :].T
    for k in range(interest_count):
        part = bil_ref[:, k * width:(k + 1) * width]
        gram[:, k * width:(k + 1) * width] = lax.dot_general(
            part, part, (((1,), (1,)), ((), ())), preferred_element_type=f32).astype(bf16)
    slot_acc[...] = jnp.zeros_like(slot_acc)
    vcat[...] = jnp.zeros_like(vcat)
    vecs[...] = jnp.zeros_like(vecs)

    slot_iota = lax.broadcasted_iota(jnp.int32, (cap, lanes), 0)

    def col_user(lane):
        return (lane // group_lanes) * GROUP_USERS + lane % GROUP_USERS

    diag = col_user(lax.broadcasted_iota(jnp.int32, (users, lanes), 1)) == lax.broadcasted_iota(jnp.int32, (users, lanes), 0)
    lane_k = (lax.broadcasted_iota(jnp.int32, (width, lanes), 1) // GROUP_USERS) % interest_count
    half_lane = lax.broadcasted_iota(jnp.int32, (OCTET, 128), 1)
    diag_g = (lax.broadcasted_iota(jnp.int32, (GROUP_USERS, mix_lanes), 1) % GROUP_USERS
              == lax.broadcasted_iota(jnp.int32, (GROUP_USERS, mix_lanes), 0))
    pos_iota = lax.broadcasted_iota(jnp.int32, (OCTET, lanes), 0)

    def place(i):
        return meta_ref[i], meta_ref[pair_max + i]

    def flat(i):
        return pl.ds(pl.multiple_of(i * OCTET, OCTET), OCTET)

    def pair_at(i):
        return pl.ds(pl.multiple_of(i * pair_rows, pair_rows), pair_rows)

    def indicator(orow16, o):
        return jnp.where(orow16 == o, 1.0, 0.0).astype(bf16)

    def over_interests(v):
        parts = []
        for h in range(0, lanes, 128):
            s = v[:, h:h + 128]
            step = group_lanes // 2
            while step >= GROUP_USERS:
                low = half_lane % (2 * step) < step
                s = s + jnp.where(low, pltpu.roll(s, 128 - step, 1), pltpu.roll(s, step, 1))
                step //= 2
            parts.append(s)
        return jnp.concatenate(parts, axis=1)

    def softmax(v):
        e = jnp.exp(v)
        return e / over_interests(e)

    def by_interest(b, mat_ref, v):
        zero = jnp.zeros_like(v)
        for k in range(interest_count):
            stack[b, k * width:(k + 1) * width, :] = jnp.where(lane_k == k, v, zero).astype(bf16)
        return dot(mat_ref[...], stack[b])

    def squash_parts(n):
        root = jnp.sqrt(n + squash_eps)
        fac = root / (1.0 + n)
        slope = (0.5 * (1.0 + n) / root - root) / ((1.0 + n) * (1.0 + n))
        return fac, 2.0 * slope

    def keep_vec(b, vec_t, j):
        vb = vec_t.astype(bf16)
        vecs[b] = vb
        vn = vb.T
        for g in range(groups):
            vcat[b, g, j * group_lanes:(j + 1) * group_lanes, :] = vn[g * group_lanes:(g + 1) * group_lanes, :]

    def build(i, j, buf):
        b, o8 = place(i)
        row = 2 * o8 + j
        crow = slot_ref[b, pl.ds(row, 1), :]
        orow16 = jnp.broadcast_to(owner_ref[b, pl.ds(row, 1), :], (16, lanes))
        lo = jnp.where(slot_iota == crow, 1.0, 0.0).astype(bf16)
        lo_ref[2 * i + j] = lo
        lo3 = lo.reshape(cap // 16, 16, lanes)
        for o in range(owners):
            buf[o * cap:(o + 1) * cap, :] = (lo3 * indicator(orow16, o)[None]).reshape(cap, lanes)

    def gather(i, j, buf):
        xtb = dot(fetched_t[...], buf[...]).astype(bf16)
        xt_ref[i, :, j * lanes:(j + 1) * lanes] = xtb
        start = pl.multiple_of(i * pair_rows + j * lanes, lanes)
        x_ref[pl.ds(start, lanes), :] = xtb.T

    pairs = chunk_count * PAIRS
    build(0, 0, oht_a)

    def gather_pair(i, carry):
        build(i, 1, oht_b)
        gather(i, 0, oht_a)
        build(jnp.minimum(i + 1, pairs - 1), 0, oht_a)
        gather(i, 1, oht_b)
        return carry

    lax.fori_loop(0, pairs, gather_pair, 0)

    def over_pairs(body):
        sums[...] = jnp.zeros_like(sums)

        def step(c, carry):
            work = []
            for q in range(PAIRS):
                i = c * PAIRS + q
                b, o8 = place(i)
                live = pos_iota + o8 * OCTET < lens_ref[pl.ds(b, 1), :]
                work.append((i, b, o8, live))
            coef = body(work)
            for q, (i, b, o8, live) in enumerate(work):
                for l in range(OCTET):
                    row = jnp.broadcast_to(coef[q][l:l + 1, :], (users, lanes))
                    mix[q, l * users:(l + 1) * users, :] = jnp.where(diag, row, 0.0).astype(bf16)
            for q, (i, b, o8, live) in enumerate(work):
                sums[b] += dot(xt_ref[i], mix[q])
            return carry

        lax.fori_loop(0, chunk_count, step, 0)

    def agreement(i, b, live):
        rows = []
        prod = dot(x_ref[pair_at(i), :], vecs[b])
        for l in range(OCTET):
            part = jnp.where(diag, prod[l * users:(l + 1) * users, :], 0.0)
            rows.append(jnp.sum(part, axis=0, keepdims=True))
        return jnp.where(live, jnp.concatenate(rows, axis=0), 0.0)

    def weigh(i, live, logits, j):
        p = softmax(logits)
        if j > 0:
            p_ref[j - 1, flat(i), :] = p
        w = jnp.where(live, p, 0.0)
        coefs[j, flat(i), :] = w
        return w

    def first(work):
        out = []
        for i, b, o8, live in work:
            logits = logit_ref[b, flat(o8), :]
            logit_now[flat(i), :] = logits
            out.append(weigh(i, live, logits, 0))
        return out

    def later(j):
        def body(work):
            out = []
            agreed = [agreement(i, b, live) for i, b, o8, live in work]
            for a, (i, b, o8, live) in zip(agreed, work):
                logits = logit_now[flat(i), :] + a
                if j == 1:
                    logit_now[flat(i), :] = logits
                out.append(weigh(i, live, logits, j))
            return out
        return body

    def back(j_prob, j_coef, j_later):
        def body(work):
            out = []
            agreed = [agreement(i, b, live) for i, b, o8, live in work]
            for dp, (i, b, o8, live) in zip(agreed, work):
                p = p_ref[j_prob, flat(i), :]
                dl = p * (dp - over_interests(p * dp))
                if j_later is not None:
                    dl = dl + coefs[j_later, flat(i), :]
                dl = jnp.where(live, dl, 0.0)
                coefs[j_coef, flat(i), :] = dl
                out.append(dl)
            return out
        return body

    squashed = [None, None]

    def turn(j):
        parts = []
        for b in range(blocks):
            xs = sums[b]
            z = by_interest(b, gram, xs)
            n = jnp.maximum(jnp.sum(xs * z, axis=0, keepdims=True), 0.0)
            fac, slope = squash_parts(n)
            z_ref[j, b] = z
            keep_vec(b, z * fac, 3 + j)
            parts.append((fac, slope))
        squashed[j] = parts

    def turn_back(j):
        for b in range(blocks):
            dxs = sums[b]
            y = by_interest(b, gram, dxs)
            z = z_ref[j, b]
            fac, slope = squashed[j][b]
            inner = slope * jnp.sum(dxs * z, axis=0, keepdims=True)
            keep_vec(b, y * fac + z * inner, j)

    over_pairs(first)
    turn(0)
    over_pairs(later(1))
    turn(1)
    over_pairs(later(2))
    outs = [by_interest(b, bilt_ref, sums[b]) for b in range(blocks)]
    cots = []
    for b, s3 in enumerate(outs):
        fac3, slope3 = squash_parts(jnp.sum(s3 * s3, axis=0, keepdims=True))
        interests_ref[b] = (s3 * fac3).astype(bf16).T
        dc3 = cot_ref[b]
        cots.append(dc3 * fac3 + s3 * (slope3 * jnp.sum(dc3 * s3, axis=0, keepdims=True)))
    for b, ds3 in enumerate(cots):
        keep_vec(b, by_interest(b, bil_ref, ds3), 2)
    over_pairs(back(1, 4, None))
    turn_back(1)
    over_pairs(back(0, 3, 4))
    turn_back(0)

    def row_grads(c, carry):
        for q in range(PAIRS):
            i = c * PAIRS + q
            b, o8 = place(i)
            for g in range(groups):
                src = (g * group_lanes) // 128 * 128
                odd = (g * group_lanes) % 128

                def piece(j, dest):
                    x = coefs[j, flat(i), src:src + 128]
                    return x if odd == dest else pltpu.roll(x, 64, 1)

                parts = []
                for h in range(0, 5, 2):
                    high = piece(h + 1, 64) if h + 1 < 5 else jnp.zeros((OCTET, 128), f32)
                    parts.append(jnp.where(half_lane < 64, piece(h, 0), high))
                row8 = jnp.concatenate(parts, axis=1)
                for l in range(OCTET):
                    row = jnp.broadcast_to(row8[l:l + 1, :], (GROUP_USERS, mix_lanes))
                    mix_g[q * groups + g, l * GROUP_USERS:(l + 1) * GROUP_USERS, :] = (
                        jnp.where(diag_g, row, 0.0).astype(bf16))
        for q in range(PAIRS):
            i = c * PAIRS + q
            b, o8 = place(i)
            for g in range(groups):
                grads = dot(mix_g[q * groups + g], vcat[b, g]).astype(bf16)
                for l in range(OCTET):
                    start = pl.multiple_of(i * pair_rows + (l * users + g * GROUP_USERS), GROUP_USERS)
                    x_ref[pl.ds(start, GROUP_USERS), :] = grads[l * GROUP_USERS:(l + 1) * GROUP_USERS, :]
        return carry

    lax.fori_loop(0, chunk_count, row_grads, 0)

    def scatter(c, carry):
        def slot_chunk(s, carry):
            for q in range(PAIRS):
                i = c * PAIRS + q
                b, o8 = place(i)
                for j in range(2):
                    lo3 = lo_ref[2 * i + j].reshape(cap // 16, 16, lanes)
                    orow16 = jnp.broadcast_to(owner_ref[b, pl.ds(2 * o8 + j, 1), :], (16, lanes))
                    t = 2 * q + j
                    for oo in range(chunk // cap):
                        ind = indicator(orow16, s * (chunk // cap) + oo)
                        oh_rows[oo * cap:(oo + 1) * cap, t * lanes:(t + 1) * lanes] = (
                            lo3 * ind[None]).reshape(cap, lanes)
            start = pl.multiple_of(s * chunk, chunk)
            rows = pl.ds(pl.multiple_of(c * PAIRS * pair_rows, PAIRS * pair_rows), PAIRS * pair_rows)
            slot_acc[pl.ds(start, chunk), :] += dot(oh_rows[...], x_ref[rows, :])
            return carry

        return lax.fori_loop(0, slots // chunk, slot_chunk, carry)

    lax.fori_loop(0, chunk_count, scatter, 0)
    slotgrad_ref[...] = slot_acc[...].astype(bf16)


def prepare(history, lengths, init_logits, interest_grad, cap):
    users, hist_count = history.shape
    interests = init_logits.shape[2]
    width = interest_grad.shape[2]
    lanes = interests * BLOCK_USERS
    blocks = users // BLOCK_USERS
    octets = -(-hist_count // OCTET)
    positions = octets * OCTET
    index = lax.iota(jnp.int32, users)
    ahead = (lengths[None, :] > lengths[:, None]) | (
        (lengths[None, :] == lengths[:, None]) & (index[None, :] < index[:, None]))
    rank = jnp.sum(ahead.astype(jnp.int32), axis=1)
    order = (rank[:, None] == index[None, :]).astype(bf16)
    column = lax.iota(jnp.int32, users * interests)
    block, rest = column // lanes, column % lanes
    group_lanes = interests * GROUP_USERS
    user = block * BLOCK_USERS + rest // group_lanes * GROUP_USERS + rest % GROUP_USERS
    interest = rest // GROUP_USERS % interests
    select = ((rank[:, None, None] == user[None, None, :])
              & (lax.iota(jnp.int32, interests)[None, :, None] == interest[None, None, :]))
    select = select.reshape(users * interests, users * interests)
    by_k = ((rank[None, :, None] == user[None, None, :])
            & (lax.iota(jnp.int32, interests)[:, None, None] == interest[None, None, :]))
    by_k = by_k.reshape(users * interests, users * interests)

    def sort_positions(values):
        s = jnp.dot(values.astype(bf16).T, order, preferred_element_type=f32).astype(jnp.int32)
        s = jnp.pad(s, ((0, positions - hist_count), (0, 0)))
        s = s.reshape(positions // TILE_POSITIONS, TILE_POSITIONS, blocks, BLOCK_USERS).transpose(2, 0, 1, 3)
        s = s.reshape(blocks, positions // TILE_POSITIONS, TILE_POSITIONS * BLOCK_USERS)
        return jnp.pad(s, ((0, 1), (0, 0), (0, 0)))

    owner = sort_positions(history // cap)
    slot = sort_positions(history % cap)
    sorted_lens = jnp.sum(jnp.where(rank[:, None] == index[None, :], lengths[:, None], 0), axis=0)
    need = (sorted_lens[::BLOCK_USERS] + OCTET - 1) // OCTET
    upto = jnp.sum(jnp.where(lax.iota(jnp.int32, blocks)[None, :] <= lax.iota(jnp.int32, blocks)[:, None], need[None, :], 0), axis=1)
    pair_max = -(-blocks * octets // PAIRS) * PAIRS
    pair = lax.iota(jnp.int32, pair_max)
    passed = pair[:, None] >= upto[None, :]
    pair_block = jnp.sum(passed.astype(jnp.int32), axis=1)
    pair_octet = jnp.where(pair_block < blocks, pair - jnp.sum(jnp.where(passed, need[None, :], 0), axis=1), 0)
    chunks = (jnp.sum(need) + PAIRS - 1) // PAIRS
    meta = jnp.concatenate([pair_block, pair_octet, chunks[None]])
    lens = jnp.sum(jnp.where(rank[:, None] == user[None, :], lengths[:, None], 0), axis=0).reshape(blocks, lanes)
    lens = jnp.pad(lens, ((0, 1), (0, 0)))
    flat = init_logits.transpose(1, 2, 0).reshape(hist_count, interests * users)
    logits = jnp.dot(flat, by_k.astype(f32), precision=lax.Precision.HIGHEST, preferred_element_type=f32)
    logits = jnp.pad(logits, ((0, positions - hist_count), (0, lanes))).reshape(positions, blocks + 1, lanes).transpose(1, 0, 2)
    grads = interest_grad.reshape(users * interests, width)
    cot = lax.dot_general(grads.astype(bf16), select.astype(bf16), (((0,), (0,)), ((), ())), preferred_element_type=f32)
    cot = cot.reshape(width, blocks, lanes).transpose(1, 0, 2)
    return owner, slot, meta, lens, logits, cot, select


def route(fetched, bilinear, prepared, cap):
    owner, slot, meta, lens, logits, cot, select = prepared
    slots, width = fetched.shape
    blocks, _, lanes = cot.shape
    interests = bilinear.shape[1] // width
    users = lanes // interests
    groups = users // GROUP_USERS
    pair_max = (meta.shape[0] - 1) // 2
    pair_rows = OCTET * users
    mix_lanes = -(-5 * lanes // groups // 128) * 128
    bilt = bilinear.reshape(width, interests, width).transpose(2, 1, 0).reshape(width, interests * width)
    chunk = 512
    out, slot_grads = pl.pallas_call(
        functools.partial(routing_kernel, interests),
        out_shape=(
            jax.ShapeDtypeStruct((blocks, lanes, width), bf16),
            jax.ShapeDtypeStruct((slots, width), bf16),
        ),
        in_specs=[pl.BlockSpec(memory_space=pltpu.SMEM)] + [pl.BlockSpec(memory_space=pltpu.VMEM)] * 8,
        scratch_shapes=[
            pltpu.VMEM((width, slots), bf16),
            pltpu.VMEM((width, interests * width), bf16),
            pltpu.VMEM((pair_max * pair_rows, width), bf16),
            pltpu.VMEM((pair_max, width, pair_rows), bf16),
            pltpu.VMEM((pair_max * 2, cap, lanes), bf16),
            pltpu.VMEM((slots, lanes), bf16),
            pltpu.VMEM((slots, lanes), bf16),
            pltpu.VMEM((PAIRS, pair_rows, lanes), bf16),
            pltpu.VMEM((blocks + 1, width, lanes), bf16),
            pltpu.VMEM((blocks + 1, groups, mix_lanes, width), bf16),
            pltpu.VMEM((blocks, interests * width, lanes), bf16),
            pltpu.VMEM((chunk, PAIRS * pair_rows), bf16),
            pltpu.VMEM((blocks + 1, width, lanes), f32),
            pltpu.VMEM((pair_max * OCTET, lanes), f32),
            pltpu.VMEM((2, pair_max * OCTET, lanes), f32),
            pltpu.VMEM((5, pair_max * OCTET, lanes), f32),
            pltpu.VMEM((PAIRS * groups, OCTET * GROUP_USERS, mix_lanes), bf16),
            pltpu.VMEM((2, blocks, width, lanes), f32),
            pltpu.VMEM((slots, width), f32),
        ],
        compiler_params=pltpu.CompilerParams(vmem_limit_bytes=VMEM_BYTES),
    )(meta, fetched, bilinear, bilt, owner, slot, lens, logits, cot)
    capsules = jnp.dot(select.astype(bf16), out.reshape(blocks * lanes, width), preferred_element_type=f32)
    return capsules.astype(bf16).reshape(blocks * users, interests, width), slot_grads


def fetch_kernel(wanted_ref, table_ref, out_ref, staged, table32, rows32, sems):
    parts = sems.shape[0]
    part = table_ref.shape[0] // parts
    copies = [
        pltpu.make_async_copy(table_ref.at[pl.ds(p * part, part), :], staged.at[pl.ds(p * part, part), :], sems.at[p])
        for p in range(parts)
    ]
    for copy in copies:
        copy.start()
    for p in range(parts):
        copies[p].wait()

        def widen(i, carry):
            base = pl.multiple_of(p * part + i * 128, 128)
            table32[pl.ds(base, 128), :] = staged[pl.ds(base, 128), :].astype(f32)
            return carry

        lax.fori_loop(0, part // 128, widen, 0)

    def copy_rows(i, carry):
        base = pl.multiple_of(i * 8, 8)
        rows = [table32[pl.ds(wanted_ref[base + j], 1), :] for j in range(8)]
        rows32[pl.ds(base, 8), :] = jnp.concatenate(rows, axis=0)
        return carry

    lax.fori_loop(0, out_ref.shape[0] // 8, copy_rows, 0, unroll=2)
    out_ref[...] = rows32[...].astype(bf16)


def fetch_rows(table, wanted):
    table_rows, width = table.shape
    count = wanted.shape[0]
    return pl.pallas_call(
        fetch_kernel,
        out_shape=jax.ShapeDtypeStruct((count, width), bf16),
        in_specs=[pl.BlockSpec(memory_space=pltpu.SMEM), pl.BlockSpec(memory_space=pl.ANY)],
        scratch_shapes=[
            pltpu.VMEM((table_rows, width), bf16),
            pltpu.VMEM((table_rows, width), f32),
            pltpu.VMEM((count, width), f32),
            pltpu.SemaphoreType.DMA((COPIES,)),
        ],
        compiler_params=pltpu.CompilerParams(vmem_limit_bytes=VMEM_BYTES),
    )(wanted, table)


def table_kernel(target_ref, rows_ref, out_ref, acc, sems):
    count = rows_ref.shape[0]
    parts = sems.shape[0]
    part = out_ref.shape[0] // parts
    acc[...] = jnp.zeros_like(acc)

    def step(i, carry):
        base = pl.multiple_of(i * 16, 16)
        rows = rows_ref[pl.ds(base, 16), :].astype(f32)
        where = [target_ref[base + j] for j in range(16)]
        for q in range(0, 16, GROUP_ROWS):
            sums = [acc[pl.ds(where[j], 1), :] + rows[j:j + 1, :] for j in range(q, q + GROUP_ROWS)]
            for j in range(q, q + GROUP_ROWS):
                acc[pl.ds(where[j], 1), :] = sums[j - q]
        return carry

    lax.fori_loop(0, count // 16, step, 0, unroll=2)
    copies = [
        pltpu.make_async_copy(acc.at[pl.ds(p * part, part), :], out_ref.at[pl.ds(p * part, part), :], sems.at[p])
        for p in range(parts)
    ]
    for copy in copies:
        copy.start()
    for copy in copies:
        copy.wait()


def add_to_table(returned, wanted, table_rows):
    count, width = returned.shape
    spare = table_rows + lax.rem(lax.broadcasted_iota(jnp.int32, (count,), 0), GROUP_ROWS)
    targets = jnp.where(wanted >= 0, wanted, spare)
    return pl.pallas_call(
        table_kernel,
        out_shape=jax.ShapeDtypeStruct((table_rows, width), f32),
        in_specs=[pl.BlockSpec(memory_space=pltpu.SMEM), pl.BlockSpec(memory_space=pltpu.VMEM)],
        out_specs=pl.BlockSpec(memory_space=pl.ANY),
        scratch_shapes=[
            pltpu.VMEM((table_rows + GROUP_ROWS, width), f32),
            pltpu.SemaphoreType.DMA((COPIES,)),
        ],
        compiler_params=pltpu.CompilerParams(vmem_limit_bytes=VMEM_BYTES),
    )(targets, returned)


def exchange(x):
    return lax.all_to_all(x, AXES, split_axis=0, concat_axis=0, tiled=True)


def local(item_table, bilinear, requests, history, lengths, init_logits, interest_grad):
    asked_ids = requests[0]
    owner_count, slot_count = asked_ids.shape
    local_table_rows, width = item_table.shape
    wanted = exchange(asked_ids)
    found = fetch_rows(item_table, jnp.maximum(wanted, 0).reshape(-1))
    found, history, lengths, init_logits, interest_grad, bilinear = lax.optimization_barrier(
        (found, history, lengths, init_logits, interest_grad, bilinear))
    fetched = exchange(found.reshape(owner_count, slot_count, width)).reshape(owner_count * slot_count, width)
    prepared = prepare(history, lengths, init_logits, interest_grad, slot_count)
    capsules, slot_grads = route(fetched, bilinear, prepared, slot_count)
    returned = exchange(slot_grads.reshape(owner_count, slot_count, width)).reshape(owner_count * slot_count, width)
    table_grad = add_to_table(returned, wanted.reshape(-1), local_table_rows)
    return capsules, table_grad


def solution(mesh):
    placed = (
        P(AXES, None),
        P(),
        P(AXES, None, None),
        P(AXES, None),
        P(AXES),
        P(AXES, None, None),
        P(AXES, None, None),
    )
    return jax.shard_map(
        local,
        mesh=mesh,
        in_specs=placed,
        out_specs=(P(AXES, None, None), P(AXES, None)),
        check_vma=False,
    )
```

time: 173 us -> 162 us (0.936); the launches traced: 174 us -> 161 us
  Pallas kernels: 93.1 us -> 80.2 us
  waiting for transfers between devices: 34.9 us -> 38.3 us
  starting transfers between devices: 16.7 us -> 13.5 us
    pallas_call x1, Pallas kernels: 74.8 us -> 61.9 us  [route(): pl.pallas_call(functools.partial(routing_kernel, interests), out_shape=(j...]
    reshape x10 -> x9, local copies, waits for them, and re-layouts: 5 us -> 1.28 us  [the longest x1 0.74 us: prepare(): jnp.pad(logits, ((0, positions - hist_count), (0, lanes)))]
    all_to_all x3, waiting for transfers between devices: 34.9 us -> 38.3 us  [exchange(): return lax.all_to_all(x, AXES, split_axis=0, concat_axis=0, tiled=True)]
    all_to_all x3, starting transfers between devices: 16.7 us -> 13.5 us  [exchange(): return lax.all_to_all(x, AXES, split_axis=0, concat_axis=0, tiled=True)]
    pad x1 -> x4, local copies, waits for them, and re-layouts: 0.02 us -> 1.89 us  [the longest x2 1.27 us: sort_positions(): return jnp.pad(s, ((0, 1), (0, 0), (0, 0)))]
  transfers between devices with their start and end apart: 3 -> 3, of which waited for: 3 -> 3; matrix products, arithmetic and copies ran while one was open for 14% -> 13% of each run, Pallas kernels for 0% -> 0%
where the time goes in v3:
time: 162 us; the launch traced here: 161 us
  Pallas kernels  80.2 us (50%)
  waiting for transfers between devices  38.3 us (24%)
  starting transfers between devices  13.5 us (8%)
  local copies, waits for them, and re-layouts  11.7 us (7%)
  other arithmetic  8.34 us (5%)
  matrix products  7.28 us (4%)
  between operations  1.73 us (1%)
    pallas_call x1, Pallas kernels, route(): pl.pallas_call(functools.partial(routing_kernel, interests), out_shape=(j...  61.9 us
    all_to_all x3, waiting for transfers between devices, exchange(): return lax.all_to_all(x, AXES, split_axis=0, concat_axis=0, tiled=True)  38.3 us
    all_to_all x3, starting transfers between devices, exchange(): return lax.all_to_all(x, AXES, split_axis=0, concat_axis=0, tiled=True)  13.5 us
    pallas_call x1, Pallas kernels, add_to_table(): pl.pallas_call(table_kernel, out_shape=jax.ShapeDtypeStruct((table_rows,...  9.45 us
    pallas_call x1, Pallas kernels, fetch_rows(): pl.pallas_call(fetch_kernel, out_shape=jax.ShapeDtypeStruct((count, width...  8.82 us
  transfers between devices with their start and end apart: 3, of which 3 were waited for; matrix products, arithmetic and copies ran while one was open for 13% of the time, Pallas kernels for 0%

profile of v3, /device:TPU:0, one launch (start us, length us, event | category | flops | bytes accessed | tf_op | source)
XLA Modules:
  0.0 161.1 jit_solution(4968071291718707461)
XLA Ops:
  0.7 7.3 %all-to-all-start = ((s32[32,1,64]{2,1,0:T(1,128)}), s32[32,1,64]{2,1,0:T(1,128)S(1)}, u32[]{:S(2)}, u32[]{:S(2)}) async-start(s32[32,1,64]{2,1,0:T(1,128)} %bitcast.52), calls=%async_computation | async-start | bytes 32768 | tf_op jit(solution)/shard_map/all_to_all | solution.py:511
  8.1 7.1 %all-to-all-done = s32[32,1,64]{2,1,0:T(1,128)S(1)} async-done(((s32[32,1,64]{2,1,0:T(1,128)}), s32[32,1,64]{2,1,0:T(1,128)S(1)}, u32[]{:S(2)}, u32[]{:S(2)}) %all-to-all-start) | async-done | bytes 8224 | tf_op jit(solution)/shard_map/all_to_all | solution.py:511
  17.0 8.8 %shard_map.86 = bf16[2048,256]{1,0:T(8,128)(2,1)} custom-call(s32[2048]{0:T(1024)} %get-tuple-element.23.wanted_ref, bf16[8192,256]{1,0:T(8,128)(2,1)} %table_ref.1), custom_call_target="tpu_custom_call" | custom-call | tf_op jit(solution)/shard_map/pallas_call | solution.py:452
  25.8 0.9 convert_reduce_fusion
  29.0 2.7 %all-to-all-start.1 = ((bf16[32,64,256]{2,1,0:T(8,128)(2,1)}), bf16[32,64,256]{2,1,0:T(8,128)(2,1)S(1)}, u32[]{:S(2)}, u32[]{:S(2)}) async-start(bf16[32,64,256]{2,1,0:T(8,128)(2,1)} %bitcast.40), calls=%async_computation.1 | async-start | bytes 2097152 | tf_op jit(solution)/shard_map/all_to_all | solution.py:511
  31.7 1.1 convolution_convert_fusion.1
  32.7 0.9 select_reduce_fusion
  36.6 1.4 fusion.4
  38.8 1.4 convert_element_type.39
  40.2 0.9 convert_element_type.40
  42.2 0.9 copy.47
  43.1 1.2 broadcast_and_fusion
  44.3 1.0 and.186
  45.3 1.2 copy.45
  47.3 2.8 %convolution_bitcast_fusion.cot_ref = f32[4,256,256]{2,1,0:T(8,128)} fusion(pred[4,256,1024]{2,1,0:T(32,128)(4,1)S(1)} %bitcast.48, bf16[1024,256]{1,0:T(8,128)(2,1)} %convert_element_type.40), kind=kOutput, calls=%fused_computation.5 | convolution fusion | flops 536870912 | bytes 2621440 | tf_op jit(solution)/shard_map/dot_general | solution.py:369
  50.1 7.8 %all-to-all-done.1 = bf16[32,64,256]{2,1,0:T(8,128)(2,1)S(1)} async-done(((bf16[32,64,256]{2,1,0:T(8,128)(2,1)}), bf16[32,64,256]{2,1,0:T(8,128)(2,1)S(1)}, u32[]{:S(2)}, u32[]{:S(2)}) %all-to-all-start.1) | async-done | bytes 1048608 | tf_op jit(solution)/shard_map/all_to_all | solution.py:511
  57.9 1.0 copy-done
  58.8 61.9 %shard_map.87 = (bf16[4,256,256]{2,1,0:T(8,128)(2,1)}, bf16[2048,256]{1,0:T(8,128)(2,1)}) custom-call(s32[57]{0:T(128)} %pad_add_fusion.meta_ref, bf16[2048,256]{1,0:T(8,128)(2,1)} %bitcast.42, bf16[256,1024]{1,0:T(8,128)(2,1)} %bil_ref, bf16[256,1024]{1,0:T(8,128)(2,1)} %bitcast.45, s32[5,14,256]{2,1,0:T(8,128)} %pad.23.owner_ref, ...), custom_call_target="tpu_custom_call" | custom-call | tf_op jit(solution)/shard_map/pallas_call | solution.py:386
  120.8 3.5 %all-to-all-start.2 = ((bf16[32,64,256]{2,1,0:T(8,128)(2,1)}), bf16[32,64,256]{2,1,0:T(8,128)(2,1)S(1)}, u32[]{:S(2)}, u32[]{:S(2)}) async-start(bf16[32,64,256]{2,1,0:T(8,128)(2,1)} %bitcast.49), calls=%async_computation.2 | async-start | bytes 2097152 | tf_op jit(solution)/shard_map/all_to_all | solution.py:511
  124.3 1.8 %convolution_convert_fusion = bf16[1024,256]{1,0:T(8,128)(2,1)S(1)} fusion(pred[1024,1024]{1,0:T(32,128)(4,1)S(1)} %and.186, bf16[1024,256]{1,0:T(8,128)(2,1)} %bitcast.53), kind=kOutput, calls=%fused_computation.6 | convolution fusion | flops 537133056 | bytes 2097152 | tf_op jit(solution)/shard_map/dot_general | solution.py:416
  126.1 0.9 reshape.318
  127.0 23.5 %all-to-all-done.2 = bf16[32,64,256]{2,1,0:T(8,128)(2,1)S(1)} async-done(((bf16[32,64,256]{2,1,0:T(8,128)(2,1)}), bf16[32,64,256]{2,1,0:T(8,128)(2,1)S(1)}, u32[]{:S(2)}, u32[]{:S(2)}) %all-to-all-start.2) | async-done | bytes 1048608 | tf_op jit(solution)/shard_map/all_to_all | solution.py:511
  150.5 1.0 copy-done.1
  151.5 9.4 %shard_map.88 = f32[8192,256]{1,0:T(8,128)} custom-call(s32[2048]{0:T(1024)} %get-tuple-element.22.target_ref, bf16[2048,256]{1,0:T(8,128)(2,1)} %bitcast.43), custom_call_target="tpu_custom_call" | custom-call | tf_op jit(solution)/shard_map/pallas_call | solution.py:497
  (42 shorter events, 9.0 us)
Async XLA Ops:
  0.6 35.9 %copy-start.3 = (f32[256,50,4]{0,2,1:T(4,128)S(1)}, f32[256,50,4]{0,2,1:T(4,128)}, u32[]{:S(2)}) copy-start(f32[256,50,4]{0,2,1:T(4,128)} %param.12) | copy-start | bytes 614404
  0.6 34.5 %copy-start.4 = (s32[256,50]{0,1:T(8,128)S(1)}, s32[256,50]{0,1:T(8,128)}, u32[]{:S(2)}) copy-start(s32[256,50]{0,1:T(8,128)} %param.10) | copy-start | bytes 153604
  0.7 40.5 %copy-start.2 = (bf16[256,1024]{1,0:T(8,128)(2,1)S(1)}, bf16[256,1024]{1,0:T(8,128)(2,1)}, u32[]{:S(2)}) copy-start(bf16[256,1024]{1,0:T(8,128)(2,1)} %bil_ref) | copy-start | bytes 1572868
  0.7 14.4 %all-to-all-start = ((s32[32,1,64]{2,1,0:T(1,128)}), s32[32,1,64]{2,1,0:T(1,128)S(1)}, u32[]{:S(2)}, u32[]{:S(2)}) async-start(s32[32,1,64]{2,1,0:T(1,128)} %bitcast.52), calls=%async_computation | async-start | bytes 32768 | tf_op jit(solution)/shard_map/all_to_all | solution.py:511
  29.0 28.9 %all-to-all-start.1 = ((bf16[32,64,256]{2,1,0:T(8,128)(2,1)}), bf16[32,64,256]{2,1,0:T(8,128)(2,1)S(1)}, u32[]{:S(2)}, u32[]{:S(2)}) async-start(bf16[32,64,256]{2,1,0:T(8,128)(2,1)} %bitcast.40), calls=%async_computation.1 | async-start | bytes 2097152 | tf_op jit(solution)/shard_map/all_to_all | solution.py:511
  57.9 1.0 copy-start
  120.8 29.7 %all-to-all-start.2 = ((bf16[32,64,256]{2,1,0:T(8,128)(2,1)}), bf16[32,64,256]{2,1,0:T(8,128)(2,1)S(1)}, u32[]{:S(2)}, u32[]{:S(2)}) async-start(bf16[32,64,256]{2,1,0:T(8,128)(2,1)} %bitcast.49), calls=%async_computation.2 | async-start | bytes 2097152 | tf_op jit(solution)/shard_map/all_to_all | solution.py:511
  150.5 1.0 copy-start.1

commit v4 on v3

--- a/solution.py
+++ b/solution.py
@@ -382,7 +382,7 @@
     pair_rows = OCTET * users
     mix_lanes = -(-5 * lanes // groups // 128) * 128
     bilt = bilinear.reshape(width, interests, width).transpose(2, 1, 0).reshape(width, interests * width)
-    chunk = 512
+    chunk = 1024 if slots <= 2048 else 512
     out, slot_grads = pl.pallas_call(
         functools.partial(routing_kernel, interests),
         out_shape=(
@@ -517,8 +517,8 @@
     local_table_rows, width = item_table.shape
     wanted = exchange(asked_ids)
     found = fetch_rows(item_table, jnp.maximum(wanted, 0).reshape(-1))
-    found, history, lengths, init_logits, interest_grad, bilinear = lax.optimization_barrier(
-        (found, history, lengths, init_logits, interest_grad, bilinear))
+    found, history, init_logits, interest_grad, bilinear = lax.optimization_barrier(
+        (found, history, init_logits, interest_grad, bilinear))
     fetched = exchange(found.reshape(owner_count, slot_count, width)).reshape(owner_count * slot_count, width)
     prepared = prepare(history, lengths, init_logits, interest_grad, slot_count)
     capsules, slot_grads = route(fetched, bilinear, prepared, slot_count)

time: 162 us -> 158 us (0.975)
  waiting for transfers between devices: 38.3 us -> 32.6 us
  local copies, waits for them, and re-layouts: 11.7 us -> 13.8 us
    all_to_all x3, waiting for transfers between devices: 38.3 us -> 32.6 us  [exchange(): return lax.all_to_all(x, AXES, split_axis=0, concat_axis=0, tiled=True)]
  transfers between devices with their start and end apart: 3 -> 3, of which waited for: 3 -> 3; matrix products, arithmetic and copies ran while one was open for 13% -> 17% of each run, Pallas kernels for 0% -> 0%
where the time goes in v4:
time: 158 us; the launch traced here: 157 us
  Pallas kernels  79.2 us (50%)
  waiting for transfers between devices  32.6 us (21%)
  local copies, waits for them, and re-layouts  13.8 us (9%)
  starting transfers between devices  13.6 us (9%)
  other arithmetic  8.34 us (5%)
  matrix products  7.73 us (5%)
  between operations  1.68 us (1%)
    pallas_call x1, Pallas kernels, route(): pl.pallas_call(functools.partial(routing_kernel, interests), out_shape=(j...  61 us
    all_to_all x3, waiting for transfers between devices, exchange(): return lax.all_to_all(x, AXES, split_axis=0, concat_axis=0, tiled=True)  32.6 us
    all_to_all x3, starting transfers between devices, exchange(): return lax.all_to_all(x, AXES, split_axis=0, concat_axis=0, tiled=True)  13.6 us
    pallas_call x1, Pallas kernels, add_to_table(): pl.pallas_call(table_kernel, out_shape=jax.ShapeDtypeStruct((table_rows,...  9.45 us
    pallas_call x1, Pallas kernels, fetch_rows(): pl.pallas_call(fetch_kernel, out_shape=jax.ShapeDtypeStruct((count, width...  8.82 us
  transfers between devices with their start and end apart: 3, of which 3 were waited for; matrix products, arithmetic and copies ran while one was open for 17% of the time, Pallas kernels for 0%

profile of v4, /device:TPU:0, one launch (start us, length us, event | category | flops | bytes accessed | tf_op | source)
XLA Modules:
  0.0 157.0 jit_solution(15497878785122452093)
XLA Ops:
  0.6 7.3 %all-to-all-start = ((s32[32,1,64]{2,1,0:T(1,128)}), s32[32,1,64]{2,1,0:T(1,128)S(1)}, u32[]{:S(2)}, u32[]{:S(2)}) async-start(s32[32,1,64]{2,1,0:T(1,128)} %bitcast.52), calls=%async_computation | async-start | bytes 32768 | tf_op jit(solution)/shard_map/all_to_all | solution.py:511
  8.0 0.9 convert_reduce_fusion
  11.4 3.6 %all-to-all-done = s32[32,1,64]{2,1,0:T(1,128)S(1)} async-done(((s32[32,1,64]{2,1,0:T(1,128)}), s32[32,1,64]{2,1,0:T(1,128)S(1)}, u32[]{:S(2)}, u32[]{:S(2)}) %all-to-all-start) | async-done | bytes 8224 | tf_op jit(solution)/shard_map/all_to_all | solution.py:511
  17.0 8.8 %shard_map.86 = bf16[2048,256]{1,0:T(8,128)(2,1)} custom-call(s32[2048]{0:T(1024)} %get-tuple-element.21.wanted_ref, bf16[8192,256]{1,0:T(8,128)(2,1)} %table_ref.1), custom_call_target="tpu_custom_call" | custom-call | tf_op jit(solution)/shard_map/pallas_call | solution.py:452
  25.8 2.7 %all-to-all-start.1 = ((bf16[32,64,256]{2,1,0:T(8,128)(2,1)}), bf16[32,64,256]{2,1,0:T(8,128)(2,1)S(1)}, u32[]{:S(2)}, u32[]{:S(2)}) async-start(bf16[32,64,256]{2,1,0:T(8,128)(2,1)} %bitcast.40), calls=%async_computation.1 | async-start | bytes 2097152 | tf_op jit(solution)/shard_map/all_to_all | solution.py:511
  28.5 0.9 select_reduce_fusion
  29.9 1.2 broadcast_and_fusion
  31.2 1.0 and.186
  32.2 2.2 %copy.45 = pred[1024,1024]{1,0:T(32,128)(4,1)} copy(pred[1024,1024]{0,1:T(32,128)(4,1)S(1)} %bitcast.41) | data formatting | bytes 2097152 | tf_op jit(solution)/shard_map/dot_general | solution.py:369
  35.2 2.4 %fusion.4 = f32[50,1024]{1,0:T(8,128)S(1)} fusion(pred[4,1024]{1,0:T(4,128)(4,1)S(1)} %iota_compare_fusion.4, pred[256,1024]{1,0:T(8,128)(4,1)S(1)} %broadcast_compare_fusion, f32[50,4,256]{2,1,0:T(4,128)} %bitcast.54), kind=kOutput, calls=%fused_computation.7 | convolution fusion | flops 630194176 | bytes 675840 | tf_op jit(solution)/shard_map/dot_general | solution.py:366
  40.8 1.4 convert_element_type.39
  42.2 0.9 convert_element_type.40
  43.1 1.4 reshape.309
  45.2 0.9 copy.47
  46.1 3.1 %convolution_bitcast_fusion.cot_ref = f32[4,256,256]{2,1,0:T(8,128)} fusion(pred[4,256,1024]{2,1,0:T(32,128)(4,1)} %bitcast.48, bf16[1024,256]{1,0:T(8,128)(2,1)} %convert_element_type.40), kind=kOutput, calls=%fused_computation.5 | convolution fusion | flops 536870912 | bytes 2621440 | tf_op jit(solution)/shard_map/dot_general | solution.py:369
  49.2 5.5 %all-to-all-done.1 = bf16[32,64,256]{2,1,0:T(8,128)(2,1)S(1)} async-done(((bf16[32,64,256]{2,1,0:T(8,128)(2,1)}), bf16[32,64,256]{2,1,0:T(8,128)(2,1)S(1)}, u32[]{:S(2)}, u32[]{:S(2)}) %all-to-all-start.1) | async-done | bytes 1048608 | tf_op jit(solution)/shard_map/all_to_all | solution.py:511
  54.7 1.0 copy-done
  55.6 61.0 %shard_map.87 = (bf16[4,256,256]{2,1,0:T(8,128)(2,1)}, bf16[2048,256]{1,0:T(8,128)(2,1)}) custom-call(s32[57]{0:T(128)} %pad_add_fusion.meta_ref, bf16[2048,256]{1,0:T(8,128)(2,1)} %bitcast.42, bf16[256,1024]{1,0:T(8,128)(2,1)} %bil_ref, bf16[256,1024]{1,0:T(8,128)(2,1)} %bitcast.45, s32[5,14,256]{2,1,0:T(8,128)} %pad.23.owner_ref, ...), custom_call_target="tpu_custom_call" | custom-call | tf_op jit(solution)/shard_map/pallas_call | solution.py:386
  116.6 3.6 %all-to-all-start.2 = ((bf16[32,64,256]{2,1,0:T(8,128)(2,1)}), bf16[32,64,256]{2,1,0:T(8,128)(2,1)S(1)}, u32[]{:S(2)}, u32[]{:S(2)}) async-start(bf16[32,64,256]{2,1,0:T(8,128)(2,1)} %bitcast.49), calls=%async_computation.2 | async-start | bytes 2097152 | tf_op jit(solution)/shard_map/all_to_all | solution.py:511
  120.2 1.8 %convolution_convert_fusion = bf16[1024,256]{1,0:T(8,128)(2,1)S(1)} fusion(pred[1024,1024]{1,0:T(32,128)(4,1)S(1)} %and.186, bf16[1024,256]{1,0:T(8,128)(2,1)} %bitcast.53), kind=kOutput, calls=%fused_computation.6 | convolution fusion | flops 537133056 | bytes 2097152 | tf_op jit(solution)/shard_map/dot_general | solution.py:416
  121.9 0.9 reshape.318
  122.9 23.5 %all-to-all-done.2 = bf16[32,64,256]{2,1,0:T(8,128)(2,1)S(1)} async-done(((bf16[32,64,256]{2,1,0:T(8,128)(2,1)}), bf16[32,64,256]{2,1,0:T(8,128)(2,1)S(1)}, u32[]{:S(2)}, u32[]{:S(2)}) %all-to-all-start.2) | async-done | bytes 1048608 | tf_op jit(solution)/shard_map/all_to_all | solution.py:511
  146.4 1.0 copy-done.1
  147.4 9.4 %shard_map.88 = f32[8192,256]{1,0:T(8,128)} custom-call(s32[2048]{0:T(1024)} %get-tuple-element.20.target_ref, bf16[2048,256]{1,0:T(8,128)(2,1)} %bitcast.43), custom_call_target="tpu_custom_call" | custom-call | tf_op jit(solution)/shard_map/pallas_call | solution.py:497
  (38 shorter events, 8.9 us)
Async XLA Ops:
  0.6 37.8 %copy-start.2 = (s32[256,50]{0,1:T(8,128)S(1)}, s32[256,50]{0,1:T(8,128)}, u32[]{:S(2)}) copy-start(s32[256,50]{0,1:T(8,128)} %param.10) | copy-start | bytes 153604
  0.6 14.4 %all-to-all-start = ((s32[32,1,64]{2,1,0:T(1,128)}), s32[32,1,64]{2,1,0:T(1,128)S(1)}, u32[]{:S(2)}, u32[]{:S(2)}) async-start(s32[32,1,64]{2,1,0:T(1,128)} %bitcast.52), calls=%async_computation | async-start | bytes 32768 | tf_op jit(solution)/shard_map/all_to_all | solution.py:511
  25.8 28.9 %all-to-all-start.1 = ((bf16[32,64,256]{2,1,0:T(8,128)(2,1)}), bf16[32,64,256]{2,1,0:T(8,128)(2,1)S(1)}, u32[]{:S(2)}, u32[]{:S(2)}) async-start(bf16[32,64,256]{2,1,0:T(8,128)(2,1)} %bitcast.40), calls=%async_computation.1 | async-start | bytes 2097152 | tf_op jit(solution)/shard_map/all_to_all | solution.py:511
  54.7 1.0 copy-start
  116.6 29.8 %all-to-all-start.2 = ((bf16[32,64,256]{2,1,0:T(8,128)(2,1)}), bf16[32,64,256]{2,1,0:T(8,128)(2,1)S(1)}, u32[]{:S(2)}, u32[]{:S(2)}) async-start(bf16[32,64,256]{2,1,0:T(8,128)(2,1)} %bitcast.49), calls=%async_computation.2 | async-start | bytes 2097152 | tf_op jit(solution)/shard_map/all_to_all | solution.py:511
  146.4 1.0 copy-start.1
